TPU v7x, 128 devices: a whole 4x4x4 slice. The times are simulated.
128 devices in a mesh: rb: 2 (over core), lb: 64 (over z, y, x).
Axes of the slice: x: 4, y: 4, z: 4, core: 2. Of those that a mesh axis runs over, the one named last changes fastest.
Arguments:
- psi_start: float32 [2, 1024, 2, 2, 1024], P(None, 'lb', None, None, 'rb')
- left_env: float32 [1024, 20, 1024], P('lb')
- right_env: float32 [1024, 20, 1024], P('rb')
- mpo_pair: float32 [20, 20, 2, 2, 2, 2], replicated
Outputs:
- output 1: float32 [2, 4], replicated
- output 2: float32 [2, 4], replicated
- output 3: float32 [2, 1024, 2, 2, 1024], P(None, 'lb', None, None, 'rb')
All inputs are finite; a program needn't handle non-finite values.
Results may differ from a plain program's by a relative error of at most 0.001.
Values sent between devices are 32-bit elements.
A program may use at most 1 GiB of HBM per device.

v0:
```python
import jax
import jax.numpy as jnp
from jax import lax
from jax.sharding import PartitionSpec as P

LANCZOS_STEPS = 4
MATMUL_PREC = lax.Precision.HIGHEST


def solution(mesh):
    lb_size = mesh.shape["lb"]
    rb_size = mesh.shape["rb"]
    psi_spec = P(None, "lb", None, None, "rb")
    vec_axes = (1, 2, 3, 4)
    both_axes = ("lb", "rb")

    def apply_ham(vec_loc, left_cols, right_loc, mpo_pair):
        vec_rows = lax.all_gather(vec_loc, "lb", axis=1, tiled=True)
        left_part = jnp.einsum("alc,taijb->tlcijb", left_cols, vec_rows, precision=MATMUL_PREC, preferred_element_type=jnp.float32)
        mid_part = jnp.einsum("lrijmn,tlcijb->trcmnb", mpo_pair, left_part, precision=MATMUL_PREC, preferred_element_type=jnp.float32)
        out_part = jnp.einsum("trcmnb,brd->tcmnd", mid_part, right_loc, precision=MATMUL_PREC, preferred_element_type=jnp.float32)
        return lax.psum_scatter(out_part, "rb", scatter_dimension=4, tiled=True)

    def local_run(psi_loc, left_loc, right_loc, mpo_pair):
        elem_count = (psi_loc.size // psi_loc.shape[0]) * lb_size * rb_size

        def mean_dot(first_vec, second_vec):
            return lax.psum(jnp.sum(first_vec * second_vec, axis=vec_axes, keepdims=True), both_axes) / elem_count

        left_cols = lax.all_to_all(left_loc, "lb", 2, 0, tiled=True)
        cur_vec = psi_loc * lax.rsqrt(mean_dot(psi_loc, psi_loc))
        prev_vec = cur_vec
        alpha_list = []
        beta_list = []
        for step_idx in range(LANCZOS_STEPS):
            ham_vec = apply_ham(cur_vec, left_cols, right_loc, mpo_pair)
            alpha = mean_dot(cur_vec, ham_vec)
            residual = ham_vec - alpha * cur_vec
            if step_idx > 0:
                residual = residual - beta_list[-1] * prev_vec
            beta = jnp.sqrt(mean_dot(residual, residual))
            prev_vec = cur_vec
            cur_vec = residual / beta
            alpha_list.append(alpha)
            beta_list.append(beta)
        alpha_vals = jnp.concatenate(alpha_list, axis=1)[:, :, 0, 0, 0]
        beta_vals = jnp.concatenate(beta_list, axis=1)[:, :, 0, 0, 0]
        return alpha_vals, beta_vals, cur_vec

    return jax.shard_map(local_run, mesh=mesh, in_specs=(psi_spec, P("lb", None, None), P("rb", None, None), P()), out_specs=(P(), P(), psi_spec), check_vma=False)
```

profile of v0, /device:TPU:1, one launch (start us, length us, event | category | flops | bytes accessed | tf_op | source)
XLA Modules:
  0.0 1331.6 jit_solution(11069949977964042159)
XLA Ops:
  7.2 1.2 multiply_reduce_fusion.8
  8.4 68.6 %psum.63 = f32[2,1,1,1,1]{0,4,3,2,1:T(1,128)S(1)} all-reduce(f32[2,1,1,1,1]{0,4,3,2,1:T(1,128)S(1)} %bitcast.162), channel_id=1, replica_groups=mesh['rb'=2,'lb'=64] {'lb','rb'}, use_global_device_ids=true, to_apply=%region_1.0 | all-reduce | flops 2 | bytes 16 | tf_op jit(solution)/shard_map/psum | solution.py:28
  77.1 1.8 copy_multiply_fusion
  78.8 7.3 copy.40
  86.1 11.0 reshape.31
  97.1 5.1 all-to-all-start
  102.6 26.2 %all-to-all-done = f32[64,1,5120]{2,1,0:T(1,128)S(1)} async-done(((f32[64,1,5120]{2,1,0:T(1,128)}), f32[64,1,5120]{2,1,0:T(1,128)S(1)}, u32[]{:S(2)}, u32[]{:S(2)}) %all-to-all-start) | async-done | bytes 1310752 | tf_op jit(solution)/shard_map/all_to_all | solution.py:30
  129.3 3.8 reduce
  133.1 11.6 reshape.32
  144.7 13.5 %copy.42 = f32[64,16,20,16]{1,0,3,2:T(8,128)} copy(f32[64,16,20,16]{2,1,3,0:T(8,128)} %bitcast.151) | data formatting | bytes 2621440 | tf_op jit(solution)/shard_map/all_to_all | solution.py:30
  158.2 9.4 all_to_all.16
  167.6 21.4 %all-gather.5.cloned.1.call-done = f32[2,1024,2,2,512]{4,1,3,2,0:T(8,128)} async-done(((f32[2,16,2,2,512]{4,1,3,2,0:T(8,128)}), f32[2,1024,2,2,512]{4,1,3,2,0:T(8,128)}) %all-gather.5.cloned.1.call-update) | async-done | bytes 16777232 | tf_op jit(solution)/shard_map/all_gather | solution.py:18
  189.0 26.2 %fusion.40 = f32[2,20,16,2,2,512,1,1]{5,1,2,4,3,0,7,6:T(8,128)S(1)} fusion(f32[2,1024,2,2,512]{4,1,3,2,0:T(8,128)} %all-gather.5.cloned.1.call-done, f32[1024,20,16,1,1,1]{0,2,1,5,4,3:T(8,128)S(1)} %bitcast.152), kind=kOutput, calls=%fused_computation.32 | convolution fusion | flops 16106127360 | bytes 23330816 | tf_op jit(solution)/shard_map/alc,taijb->tlcijb/dot_general | solution.py:19
  215.2 8.4 fusion.28
  223.6 28.5 %fusion.56 = f32[2,16,2,2,1024]{4,1,3,2,0:T(8,128)} fusion(f32[512,20,1024]{2,0,1:T(8,128)} %param.6, f32[2,20,16,2,2,512]{5,1,4,3,2,0:T(8,128)S(1)} %fusion.28), kind=kOutput, calls=%fused_computation.40 | convolution fusion | flops 16106127360 | bytes 47710208 | tf_op jit(solution)/shard_map/trcmnb,brd->tcmnd/dot_general | solution.py:21
  252.2 11.0 reduce-scatter.5.cloned.1.call-done
  263.2 1.2 multiply_reduce_fusion.7
  264.4 66.7 %psum.64 = f32[2,1,1,1,1]{0,4,3,2,1:T(1,128)S(1)} all-reduce(f32[2,1,1,1,1]{0,4,3,2,1:T(1,128)S(1)} %bitcast.165), channel_id=1, replica_groups=mesh['rb'=2,'lb'=64] {'lb','rb'}, use_global_device_ids=true, to_apply=%region_4.0 | all-reduce | flops 2 | bytes 16 | tf_op jit(solution)/shard_map/psum | solution.py:28
  331.1 1.2 multiply_reduce_fusion.6
  332.2 62.6 %psum.65 = f32[2,1,1,1,1]{0,4,3,2,1:T(1,128)S(1)} all-reduce(f32[2,1,1,1,1]{0,4,3,2,1:T(1,128)S(1)} %bitcast.163), channel_id=1, replica_groups=mesh['rb'=2,'lb'=64] {'lb','rb'}, use_global_device_ids=true, to_apply=%region_6.0 | all-reduce | flops 2 | bytes 16 | tf_op jit(solution)/shard_map/psum | solution.py:28
  394.8 1.8 broadcast_divide_fusion.3
  396.7 102.1 %all-gather.7.cloned.1.call-done = f32[2,1024,2,2,512]{4,1,3,2,0:T(8,128)} async-done(((f32[2,16,2,2,512]{4,1,3,2,0:T(8,128)}), f32[2,1024,2,2,512]{4,1,3,2,0:T(8,128)}) %all-gather.7.cloned.1.call-update) | async-done | bytes 16777232 | tf_op jit(solution)/shard_map/all_gather | solution.py:18
  498.8 26.5 %fusion.43 = f32[2,20,16,2,2,512,1,1]{5,1,2,4,3,0,7,6:T(8,128)S(1)} fusion(f32[2,1024,2,2,512]{4,1,3,2,0:T(8,128)} %all-gather.7.cloned.1.call-done, f32[1024,20,16,1,1,1]{0,2,1,5,4,3:T(8,128)S(1)} %bitcast.153), kind=kOutput, calls=%fused_computation.33 | convolution fusion | flops 16106127360 | bytes 23330816 | tf_op jit(solution)/shard_map/alc,taijb->tlcijb/dot_general | solution.py:19
  525.4 8.4 fusion.31
  533.8 28.5 %fusion.61 = f32[2,16,2,2,1024]{4,1,3,2,0:T(8,128)} fusion(f32[512,20,1024]{2,0,1:T(8,128)} %param.6, f32[2,20,16,2,2,512]{5,1,4,3,2,0:T(8,128)S(1)} %fusion.31), kind=kOutput, calls=%fused_computation.41 | convolution fusion | flops 16106127360 | bytes 47710208 | tf_op jit(solution)/shard_map/trcmnb,brd->tcmnd/dot_general | solution.py:21
  562.3 11.0 reduce-scatter.7.cloned.1.call-done
  573.3 1.1 multiply_reduce_fusion.5
  574.4 66.5 %psum.66 = f32[2,1,1,1,1]{0,4,3,2,1:T(1,128)S(1)} all-reduce(f32[2,1,1,1,1]{0,4,3,2,1:T(1,128)S(1)} %bitcast.164), channel_id=1, replica_groups=mesh['rb'=2,'lb'=64] {'lb','rb'}, use_global_device_ids=true, to_apply=%region_9.0 | all-reduce | flops 2 | bytes 16 | tf_op jit(solution)/shard_map/psum | solution.py:28
  640.9 1.2 multiply_reduce_fusion.4
  642.1 62.8 %psum.67 = f32[2,1,1,1,1]{0,4,3,2,1:T(1,128)S(1)} all-reduce(f32[2,1,1,1,1]{0,4,3,2,1:T(1,128)S(1)} %bitcast.160), channel_id=1, replica_groups=mesh['rb'=2,'lb'=64] {'lb','rb'}, use_global_device_ids=true, to_apply=%region_11.0 | all-reduce | flops 2 | bytes 16 | tf_op jit(solution)/shard_map/psum | solution.py:28
  705.7 102.1 %all-gather.9.cloned.1.call-done = f32[2,1024,2,2,512]{4,1,3,2,0:T(8,128)} async-done(((f32[2,16,2,2,512]{4,1,3,2,0:T(8,128)}), f32[2,1024,2,2,512]{4,1,3,2,0:T(8,128)}) %all-gather.9.cloned.1.call-update) | async-done | bytes 16777232 | tf_op jit(solution)/shard_map/all_gather | solution.py:18
  807.9 26.1 %fusion.46 = f32[2,20,16,2,2,512,1,1]{5,1,2,4,3,0,7,6:T(8,128)S(1)} fusion(f32[2,1024,2,2,512]{4,1,3,2,0:T(8,128)} %all-gather.9.cloned.1.call-done, f32[1024,20,16,1,1,1]{0,2,1,5,4,3:T(8,128)S(1)} %bitcast.154), kind=kOutput, calls=%fused_computation.34 | convolution fusion | flops 16106127360 | bytes 23330816 | tf_op jit(solution)/shard_map/alc,taijb->tlcijb/dot_general | solution.py:19
  833.9 8.4 fusion.34
  842.3 28.5 %fusion.66 = f32[2,16,2,2,1024]{4,1,3,2,0:T(8,128)} fusion(f32[512,20,1024]{2,0,1:T(8,128)} %param.6, f32[2,20,16,2,2,512]{5,1,4,3,2,0:T(8,128)S(1)} %fusion.34), kind=kOutput, calls=%fused_computation.42 | convolution fusion | flops 16106127360 | bytes 47710208 | tf_op jit(solution)/shard_map/trcmnb,brd->tcmnd/dot_general | solution.py:21
  870.9 11.0 reduce-scatter.9.cloned.1.call-done
  881.9 1.2 multiply_reduce_fusion.3
  883.0 66.5 %psum.68 = f32[2,1,1,1,1]{0,4,3,2,1:T(1,128)S(1)} all-reduce(f32[2,1,1,1,1]{0,4,3,2,1:T(1,128)S(1)} %bitcast.166), channel_id=1, replica_groups=mesh['rb'=2,'lb'=64] {'lb','rb'}, use_global_device_ids=true, to_apply=%region_14.0 | all-reduce | flops 2 | bytes 16 | tf_op jit(solution)/shard_map/psum | solution.py:28
  949.5 1.2 multiply_reduce_fusion.2
  950.7 63.0 %psum.69 = f32[2,1,1,1,1]{0,4,3,2,1:T(1,128)S(1)} all-reduce(f32[2,1,1,1,1]{0,4,3,2,1:T(1,128)S(1)} %bitcast.161), channel_id=1, replica_groups=mesh['rb'=2,'lb'=64] {'lb','rb'}, use_global_device_ids=true, to_apply=%region_16.0 | all-reduce | flops 2 | bytes 16 | tf_op jit(solution)/shard_map/psum | solution.py:28
  1014.6 102.1 %all-gather.11.cloned.1.call-done = f32[2,1024,2,2,512]{4,1,3,2,0:T(8,128)} async-done(((f32[2,16,2,2,512]{4,1,3,2,0:T(8,128)}), f32[2,1024,2,2,512]{4,1,3,2,0:T(8,128)}) %all-gather.11.cloned.1.call-update) | async-done | bytes 16777232 | tf_op jit(solution)/shard_map/all_gather | solution.py:18
  1116.7 26.2 %fusion.49 = f32[2,20,16,2,2,512,1,1]{5,1,2,4,3,0,7,6:T(8,128)S(1)} fusion(f32[2,1024,2,2,512]{4,1,3,2,0:T(8,128)} %all-gather.11.cloned.1.call-done, f32[1024,20,16,1,1,1]{0,2,1,5,4,3:T(8,128)S(1)} %bitcast.155), kind=kOutput, calls=%fused_computation.35 | convolution fusion | flops 16106127360 | bytes 23330816 | tf_op jit(solution)/shard_map/alc,taijb->tlcijb/dot_general | solution.py:19
  1142.9 8.4 fusion.37
  1151.3 28.5 %fusion.71 = f32[2,16,2,2,1024]{4,1,3,2,0:T(8,128)} fusion(f32[512,20,1024]{2,0,1:T(8,128)} %param.6, f32[2,20,16,2,2,512]{5,1,4,3,2,0:T(8,128)S(1)} %fusion.37), kind=kOutput, calls=%fused_computation.43 | convolution fusion | flops 16106127360 | bytes 47710208 | tf_op jit(solution)/shard_map/trcmnb,brd->tcmnd/dot_general | solution.py:21
  1179.8 11.0 reduce-scatter.11.cloned.1.call-done
  1190.9 1.2 multiply_reduce_fusion.1
  1192.0 66.5 %psum.70 = f32[2,1,1,1,1]{0,4,3,2,1:T(1,128)S(1)} all-reduce(f32[2,1,1,1,1]{0,4,3,2,1:T(1,128)S(1)} %bitcast.167), channel_id=1, replica_groups=mesh['rb'=2,'lb'=64] {'lb','rb'}, use_global_device_ids=true, to_apply=%region_19.0 | all-reduce | flops 2 | bytes 16 | tf_op jit(solution)/shard_map/psum | solution.py:28
  1258.5 1.2 multiply_reduce_fusion
  1259.7 62.6 %psum.71 = f32[2,1,1,1,1]{0,4,3,2,1:T(1,128)S(1)} all-reduce(f32[2,1,1,1,1]{0,4,3,2,1:T(1,128)S(1)} %bitcast.159), channel_id=1, replica_groups=mesh['rb'=2,'lb'=64] {'lb','rb'}, use_global_device_ids=true, to_apply=%region_21.0 | all-reduce | flops 2 | bytes 16 | tf_op jit(solution)/shard_map/psum | solution.py:28
  (41 shorter events, 5.2 us)
Async XLA Ops:
  7.2 181.8 %all-gather.5.cloned.1.call-start = ((), (), s32[]{:S(2)}) async-start(), calls=%async_computation.5 | async-start | bytes 17039360 | tf_op jit(solution)/shard_map/all_gather | solution.py:18
  86.1 16.2 %copy-start.2 = (f32[20,20,2,2,2,2]{1,5,4,3,2,0:T(2,128)S(1)}, f32[20,20,2,2,2,2]{1,5,4,3,2,0:T(2,128)}, u32[]{:S(2)}) copy-start(f32[20,20,2,2,2,2]{1,5,4,3,2,0:T(2,128)} %param.7) | copy-start | bytes 76804
  97.1 31.7 %all-to-all-start = ((f32[64,1,5120]{2,1,0:T(1,128)}), f32[64,1,5120]{2,1,0:T(1,128)S(1)}, u32[]{:S(2)}, u32[]{:S(2)}) async-start(f32[64,1,5120]{2,1,0:T(1,128)} %reshape.31), calls=%async_computation | async-start | bytes 2621440 | tf_op jit(solution)/shard_map/all_to_all | solution.py:30
  102.3 160.9 %reduce-scatter.5.cloned.1.call-start = ((), (), s32[]{:S(2)}) async-start(), calls=%async_computation.6 | async-start | bytes 786432 | tf_op jit(solution)/shard_map/reduce_scatter | solution.py:22
  223.6 39.6 %copy-start = (f32[2,16,2,2,512]{4,3,2,1,0:T(2,128)S(1)}, f32[2,16,2,2,512]{4,3,2,1,0:T(2,128)}, u32[]{:S(2)}) copy-start(f32[2,16,2,2,512]{4,3,2,1,0:T(2,128)} %param.4) | copy-start | bytes 786436
  252.2 246.7 %all-gather.7.cloned.1.call-start = ((), (), s32[]{:S(2)}) async-start(), calls=%async_computation.7 | async-start | bytes 17039360 | tf_op jit(solution)/shard_map/all_gather | solution.py:18
  396.6 176.7 %reduce-scatter.7.cloned.1.call-start = ((), (), s32[]{:S(2)}) async-start(), calls=%async_computation.8 | async-start | bytes 786432 | tf_op jit(solution)/shard_map/reduce_scatter | solution.py:22
  533.7 39.6 %copy-start.1 = (f32[2,16,2,2,512]{4,1,3,2,0:T(8,128)S(1)}, f32[2,16,2,2,512]{4,1,3,2,0:T(8,128)}, u32[]{:S(2)}) copy-start(f32[2,16,2,2,512]{4,1,3,2,0:T(8,128)} %broadcast_divide_fusion.3) | copy-start | bytes 786436
  562.3 245.6 %all-gather.9.cloned.1.call-start = ((), (), s32[]{:S(2)}) async-start(), calls=%async_computation.9 | async-start | bytes 17039360 | tf_op jit(solution)/shard_map/all_gather | solution.py:18
  705.7 176.2 %reduce-scatter.9.cloned.1.call-start = ((), (), s32[]{:S(2)}) async-start(), calls=%async_computation.10 | async-start | bytes 786432 | tf_op jit(solution)/shard_map/reduce_scatter | solution.py:22
  870.8 245.9 %all-gather.11.cloned.1.call-start = ((), (), s32[]{:S(2)}) async-start(), calls=%async_computation.11 | async-start | bytes 17039360 | tf_op jit(solution)/shard_map/all_gather | solution.py:18
  1014.5 176.4 %reduce-scatter.11.cloned.1.call-start = ((), (), s32[]{:S(2)}) async-start(), calls=%async_computation.12 | async-start | bytes 786432 | tf_op jit(solution)/shard_map/reduce_scatter | solution.py:22
Sparse Core Ops, SparseCore 0:
  79.0 109.9 all-gather.4
  252.3 10.8 reduce-scatter.4
  396.8 102.0 all-gather.6
  562.4 10.8 reduce-scatter.6
  705.8 102.0 all-gather.8
  870.9 10.8 reduce-scatter.8
  1014.6 102.0 all-gather.10
  1180.0 10.8 reduce-scatter.10
where the time goes:
time: 1340 us; the launch traced here: 1330 us
  blocking collectives  586 us (44%)
  waiting for transfers between devices  398 us (30%)
  matrix products  253 us (19%)
  local copies, waits for them, and re-layouts  55.8 us (4%)
  other arithmetic  19.5 us (1%)
  between operations  14.5 us (1%)
    psum x9, blocking collectives, mean_dot(): lax.psum(jnp.sum(first_vec * second_vec, axis=vec_axes, keepdims=True), b...  586 us
    all_gather x4, waiting for transfers between devices, apply_ham(): vec_rows = lax.all_gather(vec_loc, 'lb', axis=1, tiled=True)  328 us
    dot_general x4, matrix products, apply_ham(): jnp.einsum('trcmnb,brd->tcmnd', mid_part, right_loc, precision=MATMUL_PRE...  114 us
    dot_general x4, matrix products, apply_ham(): jnp.einsum('alc,taijb->tlcijb', left_cols, vec_rows, precision=MATMUL_PRE...  105 us
    reduce_scatter x4, waiting for transfers between devices, apply_ham(): return lax.psum_scatter(out_part, 'rb', scatter_dimension=4, tiled=True)  44 us
    dot_general x4, matrix products, apply_ham(): jnp.einsum('lrijmn,tlcijb->trcmnb', mpo_pair, left_part, precision=MATMUL...  33.5 us
    unnamed x11, local copies, waits for them, and re-layouts  31 us
  transfers between devices with their start and end apart: 9, of which 9 were waited for; matrix products, arithmetic and copies ran while one was open for 4% of the time, Pallas kernels for 0%

commit v1 on v0

v1 whole, which is shorter than its diff:
```python
import functools

import jax
import jax.numpy as jnp
from jax import lax
from jax.experimental import pallas as pl
from jax.experimental.pallas import tpu as pltpu
from jax.sharding import PartitionSpec as P

STEPS = 4
HI = lax.Precision.HIGHEST
F32 = jnp.float32
BF16 = jnp.bfloat16
MESH = pl.DeviceIdType.MESH
LN = 128
EC = 64
PH = 4
WID = PH * LN
NX = 40
NY = 72
FAR = (7, 6, 5, 3)
NEAR = (4, 2, 1)
SEVEN = NEAR + FAR
ALPHA, BETA, NORM = range(3)
RS, GA, FW, PS, PF, FI, AG, AR, LD = range(9)
THIRDS = ((0, 4), (4, 3), (7, 3))
ORDERS = ((4, 2, 1), (2, 1, 4), (1, 4, 2))


def split3(val):
    top = val.astype(BF16)
    rest = val - top.astype(F32)
    mid = rest.astype(BF16)
    low = (rest - mid.astype(F32)).astype(BF16)
    return top, mid, low


def fold(val):
    acc = sum(val[:, j:j + LN] for j in range(0, val.shape[1], LN))
    return sum(acc[j:j + 8] for j in range(0, val.shape[0], 8))


def bits(m):
    return m // 4, (m // 2) % 2, m % 2


def number(trip, base=2):
    return (trip[0] * base + trip[1]) * base + trip[2]


def flip(trip, m):
    return number([q + b * (1 - 2 * q) for q, b in zip(trip, bits(m))])


def places(lb):
    place = (lb // 16, (lb // 4) % 4, lb % 4)
    return place, [q % 2 for q in place], [q // 2 for q in place], [((q + 1) // 2) % 2 for q in place]


def kernel(cfg, psi_ref, left_ref, right_ref, wmat_ref, psi_out, alpha_out, beta_out,
           rf, ls, lst, gat, vec, pg, praw, xf, yf, outb, rsb, wpk, gbuf, rbuf, asend, scal, fsend, frecv, ssem, rsem, l_s, l_r, lf_s, lf_r):
    bond, mpo, elems = cfg
    core, lb = lax.axis_index("rb"), lax.axis_index("lb")
    place, low, high, side = places(lb)
    pos, aset, eset = number(low), number(high), number(side)
    half = bond // 2
    own = pl.multiple_of(core * half + eset * EC, EC)
    other = 1 - core
    myrows = pl.ds(pl.multiple_of(pos * 16, 16), 16)
    mycols = pl.ds(pl.multiple_of(core * half, half), half)

    def gpeer(m):
        return number([q + b * (1 - 2 * p) for q, b, p in zip(place, bits(m), low)], 4)

    def rpeer(m):
        return number([q + b * (3 - 2 * q) for q, b in zip(place, bits(m))], 4)

    def remote(src, dst, ssm, rsm, c, chip):
        return pltpu.make_async_remote_copy(src_ref=src, dst_ref=dst, send_sem=ssm, recv_sem=rsm, device_id=(c, chip), device_id_type=MESH)

    def tagged(src, dst, kind, t, m, c, chip):
        return remote(src, dst, ssem.at[kind, t, m], rsem.at[kind, t, m], c, chip)

    def rs_copy(t, m):
        return tagged(outb.at[t, flip(high, m)], rsb.at[t, m], RS, t, m, core, rpeer(m))

    def g_copy(t, m):
        reg = gat.at[t, pl.ds(own, EC)]
        return tagged(reg, reg, GA, t, m, core, gpeer(m))

    def fw_copy(t, m):
        reg = gat.at[t, pl.ds(pl.multiple_of(core * half + flip(side, m) * EC, EC), EC)]
        return tagged(reg, reg, FW, t, m, other, lb)

    def p_copy(t, m):
        reg = pg.at[t, :, myrows, mycols]
        return tagged(reg, reg, PS, t, m, core, gpeer(m))

    def pf_copy(t):
        reg = pg.at[t, :, :, mycols]
        return tagged(reg, reg, PF, t, 0, other, lb)

    def f_copy(t, m):
        src = fsend.at[t, :, pl.ds(pl.multiple_of(flip(low, m) * 16, 16), 16)]
        return tagged(src, frecv.at[t, eset], FI, t, m, core, gpeer(m))

    def l_region(m, j):
        first, count = THIRDS[j]
        return ls.at[pl.ds(core * (mpo // 2) + first, count), pl.ds(pl.multiple_of(flip(low, m) * 16, 16), 16)]

    def l_copy(m, j, d):
        reg = l_region(m, j)
        return remote(reg, reg, l_s.at[j, m, d], l_r.at[j, m + d], core, gpeer(d))

    def lf_copy(m, j):
        reg = l_region(m, j)
        return remote(reg, reg, lf_s.at[j, m], lf_r.at[j, m], other, lb)

    group = [(c, m) for c in range(2) for m in range(8) if c or m]

    def ag_copy(t, kind, c, m):
        return remote(asend.at[kind, t, 0], gbuf.at[kind, t, core * 8 + eset], ssem.at[AG + 2 * kind, t, m + 8 * c], rsem.at[AG + 2 * kind, t, m + 8 * c], core + c * (1 - 2 * core), gpeer(m))

    def ar_copy(t, kind, m):
        return remote(asend.at[kind, t, 1], rbuf.at[kind, t, aset], ssem.at[AR + 2 * kind, t, m], rsem.at[AR + 2 * kind, t, m], core, rpeer(m))

    def g_send(t, kind, part):
        asend[kind, t, 0] = part
        gbuf[kind, t, core * 8 + eset] = part
        for c, m in group:
            ag_copy(t, kind, c, m).start()

    def g_sum(t, kind):
        for c, m in group:
            ag_copy(t, kind, c, m).wait_recv()
        return sum(gbuf[kind, t, j] for j in range(16))

    def r_send(t, kind, part):
        asend[kind, t, 1] = part
        rbuf[kind, t, aset] = part
        for m in SEVEN:
            ar_copy(t, kind, m).start()

    def r_sum(t, kind):
        for m in SEVEN:
            ar_copy(t, kind, m).wait_recv()
        return sum(rbuf[kind, t, j] for j in range(8))

    def total(t, kind, tile):
        for c, m in group:
            ag_copy(t, kind, c, m).wait_send()
        for m in SEVEN:
            ar_copy(t, kind, m).wait_send()
        return jnp.sum(jnp.sum(tile, axis=0, keepdims=True), axis=1, keepdims=True) / elems

    def put(t, kind, val):
        scal[kind, t] = jnp.broadcast_to(val, (8, LN))

    def get(t, kind):
        return scal[kind, t][0:1, 0:1]

    def record(out, t, s, val):
        rows = lax.broadcasted_iota(jnp.int32, out.shape, 0)
        cols = lax.broadcasted_iota(jnp.int32, out.shape, 1)
        out[...] = jnp.where(jnp.logical_and(rows == t, cols == s), val, out[...])

    psi_ld = pltpu.make_async_copy(psi_ref, praw, ssem.at[LD + 6, 0, 0])
    psi_ld.start()
    l_ld = pltpu.make_async_copy(left_ref, lst, ssem.at[LD + 6, 0, 1])
    l_ld.start()
    r_ld = pltpu.make_async_copy(right_ref.at[:, pl.ds(pl.multiple_of(eset * EC, EC), EC)], rf, ssem.at[LD + 6, 0, 2])
    r_ld.start()
    barrier = pltpu.get_barrier_semaphore()
    for c, m in group:
        pl.semaphore_signal(barrier, inc=1, device_id=(core + c * (1 - 2 * core), gpeer(m)), device_id_type=MESH)
    for m in SEVEN:
        pl.semaphore_signal(barrier, inc=1, device_id=(core, rpeer(m)), device_id_type=MESH)
    psi_ld.wait()
    parts = []
    for t in range(2):
        acc = 0
        for ij in range(PH):
            val = praw[t, :, ij // 2, ij % 2, :]
            pg[t, ij, myrows, mycols] = val
            acc = acc + val * val
        parts.append(fold(acc))
    alpha_out[...] = jnp.zeros(alpha_out.shape, F32)
    beta_out[...] = jnp.zeros(beta_out.shape, F32)
    pl.semaphore_wait(barrier, len(group) + len(SEVEN))
    for t in range(2):
        g_send(t, NORM, parts[t])
    for m in SEVEN:
        p_copy(0, m).start()
    l_ld.wait()

    def perm_body(l, carry):
        lane = lax.broadcasted_iota(jnp.int32, (16, LN), 1) // 32
        for hz in range(2):
            for hy in range(2):
                src = [lst[l, :, pl.ds((4 * hz + 2 * q + hy) * LN, LN)] for q in range(2)]
                for hx in range(2):
                    pick = None
                    for c in range(PH):
                        shift = (c - 2 * (c % 2) - hx) * 32 % LN
                        val = pltpu.roll(src[c // 2], shift, 1) if shift else src[c // 2]
                        pick = val if pick is None else jnp.where(lane == c, val, pick)
                    ls[l, myrows, pl.ds(number((hz, hy, hx)) * LN, LN)] = pick
        return carry

    lax.fori_loop(0, mpo, perm_body, 0)
    for j in range(3):
        for d in NEAR:
            l_copy(0, j, d).start()
    w0, w1, w2 = split3(wmat_ref[...])
    wpk[...] = jnp.concatenate([w0, w0, w0, w1, w1, w2], axis=1)
    for t in range(2):
        r_send(t, NORM, g_sum(t, NORM))

    def l_spread():
        for j in range(3):
            a, b, c = ORDERS[j]
            l_r_wait(a, j, (b, c))
            l_r_wait(b, j, (c,))
            l_r_wait(c, j, ())
        for j in range(3):
            a, b, c = ORDERS[j]
            l_r_wait(a + b, j, (c,))
        for m in SEVEN:
            p_copy(1, m).start()
        for j in range(3):
            a, b, c = ORDERS[j]
            for m in (a + c, b + c, a + b + c):
                l_r_wait(m, j, ())
        for j in range(3):
            for m in SEVEN:
                lf_copy(m, j).wait_recv()
        for j in range(3):
            a, b, c = ORDERS[j]
            for m, d in ((0, a), (0, b), (0, c), (a, b), (a, c), (b, c), (a + b, c)):
                l_copy(m, j, d).wait_send()
            for m in SEVEN:
                lf_copy(m, j).wait_send()

    def l_r_wait(m, j, links):
        l_copy_in(m, j).wait_recv()
        for d in links:
            l_copy(m, j, d).start()
        lf_copy(m, j).start()

    def l_copy_in(m, j):
        reg = l_region(m, j)
        return remote(reg, reg, l_s.at[j, 0, 0], l_r.at[j, m], core, lb)

    def ev_init(t):
        for m in SEVEN:
            p_copy(t, m).wait_recv()
        pf_copy(t).start()
        rinv = 1.0 / jnp.sqrt(total(t, NORM, r_sum(t, NORM)))
        put(t, BETA, jnp.zeros((1, 1), F32))
        pf_copy(t).wait_recv()

        def tr_body(b, carry):
            rows = pl.ds(pl.multiple_of(b * LN, LN), LN)
            for ij in range(PH):
                vec[t, 0, rows, ij * LN:(ij + 1) * LN] = pg[t, ij, :, rows].T * rinv
            vec[t, 1, rows] = jnp.zeros((LN, WID), F32)
            return carry

        lax.fori_loop(0, bond // LN, tr_body, 0)
        for m in SEVEN:
            p_copy(t, m).wait_send()
        pf_copy(t).wait_send()

    def ev_sum(t, s, more):
        for m in SEVEN:
            rs_copy(t, m).wait_recv()
        hv = outb[t, aset] + sum(rsb[t, m] for m in SEVEN)
        gat[t, pl.ds(own, EC)] = hv
        g_send(t, ALPHA, fold(hv * vec[t, s % 2, pl.ds(own, EC)]))

        @pl.when(more)
        def _():
            for m in SEVEN:
                g_copy(t, m).start()
            fw_copy(t, 0).start()

        for m in SEVEN:
            rs_copy(t, m).wait_send()

    def new_w(t, s, rows):
        return gat[t, rows] - get(t, ALPHA) * vec[t, s % 2, rows] - get(t, BETA) * vec[t, (s + 1) % 2, rows]

    def ev_mid(t):
        r_send(t, ALPHA, g_sum(t, ALPHA))

    def ev_alpha(t, s):
        alpha = total(t, ALPHA, r_sum(t, ALPHA))
        put(t, ALPHA, alpha)
        record(alpha_out, t, s, alpha)
        res = new_w(t, s, pl.ds(own, EC))
        r_send(t, BETA, fold(res * res))

    def ev_mid2(t):
        g_send(t, BETA, r_sum(t, BETA))

    def ev_fwd(t, which):
        for m in which:
            g_copy(t, m).wait_recv()
            fw_copy(t, m).start()

    def ev_beta(t, s):
        beta = jnp.sqrt(total(t, BETA, g_sum(t, BETA)))
        record(beta_out, t, s, beta)
        return beta

    def ev_vec(t, s):
        beta = ev_beta(t, s)
        rinv = 1.0 / beta

        def rows_of(first):
            def body(j, carry):
                rows = pl.ds(pl.multiple_of(first + j * LN, LN), LN)
                vec[t, (s + 1) % 2, rows] = new_w(t, s, rows) * rinv
                return carry

            lax.fori_loop(0, half // LN, body, 0)

        rows_of(core * half)
        for m in range(8):
            fw_copy(t, m).wait_recv()
        rows_of(other * half)
        put(t, BETA, beta)
        for m in range(8):
            fw_copy(t, m).wait_send()
        for m in SEVEN:
            g_copy(t, m).wait_send()

    def r_phase(t, s, first, count):
        xv = jnp.dot(rf[:, pl.ds(first, count), :].reshape(mpo * count, bond), vec[t, s % 2], preferred_element_type=F32, precision=HI)
        for r in range(mpo):
            for ij in range(PH):
                xf[pl.ds((ij * mpo + r) * NX, count), :] = xv[r * count:(r + 1) * count, ij * LN:(ij + 1) * LN]

    def w_phase(first, count):
        for e in range(0, count, 2):
            xs = jnp.concatenate([xf[pl.ds(e + q, PH * mpo, stride=NX), :] for q in range(2)], axis=1)
            x0, x1, x2 = split3(xs)
            yv = jnp.dot(wpk[...], jnp.concatenate([x0, x1, x2, x0, x1, x0], axis=0), preferred_element_type=F32)
            for q in range(2):
                yf[pl.ds(first + e + q, PH * mpo, stride=NY), :] = yv[:, q * LN:(q + 1) * LN]

    def step_body(it, carry):
        t, s = it % 2, it // 2
        ot = 1 - t
        os = (it + 1) // 2 - 1
        has = it >= 1
        more = jnp.logical_and(has, it < 2 * STEPS - 1)

        @pl.when(it < 2)
        def _():
            ev_init(t)

        @pl.when(it >= 2)
        def _():
            ev_vec(t, s - 1)

        @pl.when(it == 0)
        def _():
            r_ld.wait()

        r_phase(t, s, 0, 32)

        @pl.when(has)
        def _():
            ev_sum(ot, os, more)

        w_phase(0, 32)

        def quarter(j, c2):
            first = pl.multiple_of(32 + j * 16, 16)
            r_phase(t, s, first, 16)

            @pl.when(jnp.logical_and(has, j == 0))
            def _():
                ev_mid(ot)

            w_phase(first, 16)
            return c2

        lax.fori_loop(0, 2, quarter, 0)

        @pl.when(has)
        def _():
            ev_alpha(ot, os)

        @pl.when(more)
        def _():
            ev_fwd(ot, NEAR)

        @pl.when(it == 0)
        def _():
            l_spread()

        def l_body(n, c2):
            ms = [FAR[j] + n * ((NEAR + (0,))[j] - FAR[j]) for j in range(PH)]
            blks = [flip(high, m) for m in ms]
            lhs = jnp.concatenate([jnp.concatenate([yf[pl.ds((l * PH + mn) * NY, EC), :] for mn in range(PH)], axis=0) for l in range(mpo)], axis=1)
            rhs = jnp.concatenate([ls[:, :, pl.ds(pl.multiple_of(b * LN, LN), LN)].reshape(mpo * LN, LN) for b in blks], axis=1)
            ov = jnp.dot(lhs, rhs, preferred_element_type=F32, precision=HI)
            for j in range(PH):
                for mn in range(PH):
                    outb[t, blks[j], :, mn * LN:(mn + 1) * LN] = ov[mn * EC:(mn + 1) * EC, j * LN:(j + 1) * LN]
            for m in ms[:3]:
                rs_copy(t, m).start()

            @pl.when(n == 0)
            def _():
                rs_copy(t, FAR[3]).start()

            @pl.when(jnp.logical_and(has, n == 0))
            def _():
                ev_mid2(ot)

            @pl.when(jnp.logical_and(more, n == 0))
            def _():
                ev_fwd(ot, FAR[1:])

            @pl.when(jnp.logical_and(more, n == 1))
            def _():
                ev_fwd(ot, FAR[:1])

            return c2

        lax.fori_loop(0, 2, l_body, 0)
        return carry

    lax.fori_loop(0, 2 * STEPS, step_body, 0)

    last = STEPS - 1

    def finish(t):
        res = new_w(t, last, pl.ds(own, EC)) * (1.0 / ev_beta(t, last))
        for q in range(2):
            pair = [res[:, j * LN:(j + 1) * LN] for j in (2 * q, 2 * q + 1)]
            fsend[t, q] = jnp.concatenate(pair, axis=0).T
        for m in SEVEN:
            f_copy(t, m).start()
        frecv[t, eset] = fsend[t, :, myrows]

    def assemble(t):
        for m in SEVEN:
            f_copy(t, m).wait_recv()
        for i in range(2):
            for j in range(2):
                psi_out[t, :, i, j, :] = jnp.concatenate([frecv[t, g, i][:, j * EC:(j + 1) * EC] for g in range(8)], axis=1)
        for m in SEVEN:
            f_copy(t, m).wait_send()

    ev_sum(1, last, False)
    finish(0)
    ev_mid(1)
    assemble(0)
    ev_alpha(1, last)
    ev_mid2(1)
    finish(1)
    assemble(1)


def solution(mesh):
    psi_spec = P(None, "lb", None, None, "rb")

    def local_run(psi_loc, left_loc, right_loc, mpo_pair):
        targets, rows, phys, _, half = psi_loc.shape
        mpo, bond = left_loc.shape[1:]
        left_t = jnp.transpose(left_loc, (1, 0, 2))
        right_t = jnp.transpose(right_loc, (1, 0, 2))
        wmat = jnp.transpose(mpo_pair.reshape(mpo, mpo, PH, PH), (0, 3, 2, 1)).reshape(PH * mpo, PH * mpo)
        dma = pltpu.SemaphoreType.DMA
        any_spec = pl.BlockSpec(memory_space=pl.ANY)
        vm = pl.BlockSpec(memory_space=pltpu.VMEM)
        f32_shapes = [
            (mpo, EC, bond),
            (mpo, LN, bond),
            (mpo, rows, bond),
            (2, bond, WID),
            (2, 2, bond, WID),
            (2, PH, LN, bond),
            psi_loc.shape,
            (PH * mpo * NX, LN),
            (PH * mpo * NY, LN),
            (2, 8, EC, WID),
            (2, 8, EC, WID),
        ]
        small = [(3, 2, 16, 8, LN), (3, 2, 8, 8, LN), (3, 2, 2, 8, LN), (2, 2, 8, LN), (2, 2, LN, LN), (2, 8, 2, 16, LN)]
        call = pl.pallas_call(
            functools.partial(kernel, (bond, mpo, float(bond * bond * PH))),
            out_shape=[jax.ShapeDtypeStruct(shape, F32) for shape in (psi_loc.shape, (targets, STEPS), (targets, STEPS))],
            in_specs=[any_spec, any_spec, any_spec, vm],
            out_specs=[vm] * 3,
            scratch_shapes=[pltpu.VMEM(shape, F32) for shape in f32_shapes]
            + [pltpu.VMEM((PH * mpo, 6 * PH * mpo), BF16)]
            + [pltpu.VMEM(shape, F32) for shape in small]
            + [dma((16, 2, 16))] * 2
            + [dma((3, 8, 8)), dma((3, 8)), dma((3, 8)), dma((3, 8))],
            compiler_params=pltpu.CompilerParams(vmem_limit_bytes=63 << 20, has_side_effects=True, collective_id=0),
            name="lanczos",
        )
        psi_next, alpha_vals, beta_vals = call(psi_loc, left_t, right_t, wmat)
        return alpha_vals, beta_vals, psi_next

    return jax.shard_map(local_run, mesh=mesh, in_specs=(psi_spec, P("lb", None, None), P("rb", None, None), P()), out_specs=(P(), P(), psi_spec), check_vma=False)
```

time: 1340 us -> 346 us (0.26)
  blocking collectives: 586 us -> 0 us
  waiting for transfers between devices: 398 us -> 0 us
  Pallas kernels: 0 us -> 339 us
  matrix products: 253 us -> 0 us
  local copies, waits for them, and re-layouts: 55.8 us -> 5.83 us
  other arithmetic: 19.5 us -> 0 us
  between operations: 14.5 us -> 0.64 us
    psum x9 -> x0, blocking collectives: 586 us -> none  [mean_dot(): lax.psum(jnp.sum(first_vec * second_vec, axis=vec_axes, keepdims=True), b...]
    pallas_call x0 -> x1, Pallas kernels: none -> 339 us  [local_run(): psi_next, alpha_vals, beta_vals = call(psi_loc, left_t, right_t, wmat)]
    all_gather x4 -> x0, waiting for transfers between devices: 328 us -> none  [apply_ham(): vec_rows = lax.all_gather(vec_loc, 'lb', axis=1, tiled=True)]
    dot_general x12 -> x0, matrix products: 253 us -> none  [the longest x4 114 us: apply_ham(): jnp.einsum('trcmnb,brd->tcmnd', mid_part, right_loc, precision=MATMUL_PRE...]
    reduce_scatter x4 -> x0, waiting for transfers between devices: 44 us -> none  [apply_ham(): return lax.psum_scatter(out_part, 'rb', scatter_dimension=4, tiled=True)]
    unnamed x11 -> x3, local copies, waits for them, and re-layouts: 31 us -> 4.13 us
    all_to_all x1 -> x0, waiting for transfers between devices: 26.2 us -> none  [local_run(): left_cols = lax.all_to_all(left_loc, 'lb', 2, 0, tiled=True)]
    all_to_all x3 -> x0, local copies, waits for them, and re-layouts: 23.4 us -> none  [local_run(): left_cols = lax.all_to_all(left_loc, 'lb', 2, 0, tiled=True)]
  transfers between devices with their start and end apart: 9 -> 0, of which waited for: 9 -> 0; matrix products, arithmetic and copies ran while one was open for 4% -> 0% of each run, Pallas kernels for 0% -> 0%
where the time goes in v1:
time: 346 us
  Pallas kernels  339 us (98%)
  local copies, waits for them, and re-layouts  5.83 us (2%)
    pallas_call x1, Pallas kernels, local_run(): psi_next, alpha_vals, beta_vals = call(psi_loc, left_t, right_t, wmat)  339 us

profile of v1, /device:TPU:1, one launch (start us, length us, event | category | flops | bytes accessed | tf_op | source)
XLA Modules:
  0.0 345.9 jit_solution(13761699762789013343)
XLA Ops:
  0.6 1.0 copy.9
  1.6 0.7 reshape.13.wmat_ref
  2.3 339.5 %lanczos.1 = (f32[2,16,2,2,512]{4,3,2,1,0:T(2,128)}, f32[2,4]{1,0:T(2,128)}, f32[2,4]{1,0:T(2,128)}) custom-call(f32[2,16,2,2,512]{4,3,2,1,0:T(2,128)} %psi_ref.1, f32[20,16,1024]{2,1,0:T(8,128)} %bitcast.7, f32[20,512,1024]{2,1,0:T(8,128)} %bitcast.6, f32[80,80]{1,0:T(8,128)} %reshape.13.wmat_ref), custom_call_target="tpu_custom_call" | custom-call | tf_op jit(solution)/shard_map/lanczos/pallas_call | solution.py:508
  341.8 1.2 copy.13
  343.0 1.2 copy.14
  344.3 1.7 copy.15

commit v2 on v1

v2 whole, which is shorter than its diff:
```python
import functools

import jax
import jax.numpy as jnp
from jax import lax
from jax.experimental import pallas as pl
from jax.experimental.pallas import tpu as pltpu
from jax.sharding import PartitionSpec as P

STEPS = 4
HI = lax.Precision.HIGHEST
F32 = jnp.float32
BF16 = jnp.bfloat16
MESH = pl.DeviceIdType.MESH
LN = 128
EC = 64
EH = EC // 2
PH = 4
WID = PH * LN
NX = 40
NY = 72
FAR = (3, 5, 6, 7)
CLOSE = (4, 2, 1, 0)
NEAR = CLOSE[:3]
SEVEN = FAR + NEAR
ALPHA, BETA, NORM, FAC = range(4)
SIZE = FAC + 2
RS, GA, FW = 0, 2, 4
PS, PF, FI, AG = range(6, 10)
AR = AG + 3
LS, LF = AR + 3, AR + 4
KINDS = AR + 5
THIRDS = ((0, 4), (4, 3), (7, 3))
ORDERS = ((4, 2, 1), (2, 1, 4), (1, 4, 2))


def split3(val):
    top = val.astype(BF16)
    rest = val - top.astype(F32)
    mid = rest.astype(BF16)
    low = (rest - mid.astype(F32)).astype(BF16)
    return top, mid, low


def fold(val):
    acc = sum(val[:, j:j + LN] for j in range(0, val.shape[1], LN))
    return sum(acc[j:j + 8] for j in range(0, val.shape[0], 8))


def bits(m):
    return m // 4, (m // 2) % 2, m % 2


def number(trip, base=2):
    return (trip[0] * base + trip[1]) * base + trip[2]


def flip(trip, m):
    return number([q + b * (1 - 2 * q) for q, b in zip(trip, bits(m))])


def places(lb):
    place = (lb // 16, (lb // 4) % 4, lb % 4)
    return place, [q % 2 for q in place], [q // 2 for q in place], [((q + 1) // 2) % 2 for q in place]


def kernel(cfg, psi_ref, left_ref, right_ref, wmat_ref, psi_out, sums_out,
           rf, ls, lst, gat, vec, pg, praw, xf, yf, outb, rsb, l3, wpk, gbuf, rbuf, asend, scal, fsend, frecv, ssem, rsem, lsem, ldsem):
    bond, mpo, elems = cfg
    core, lb = lax.axis_index("rb"), lax.axis_index("lb")
    place, low, high, side = places(lb)
    pos, aset, eset = number(low), number(high), number(side)
    half, lhalf = bond // 2, mpo // 2
    own = core * half + eset * EC
    other = 1 - core
    myrows = pl.ds(pl.multiple_of(pos * 16, 16), 16)
    mycols = pl.ds(pl.multiple_of(core * half, half), half)

    def gpeer(m):
        return number([q + b * (1 - 2 * p) for q, b, p in zip(place, bits(m), low)], 4)

    def rpeer(m):
        return number([q + b * (3 - 2 * q) for q, b in zip(place, bits(m))], 4)

    def remote(src, dst, ssm, rsm, c, chip):
        return pltpu.make_async_remote_copy(src_ref=src, dst_ref=dst, send_sem=ssm, recv_sem=rsm, device_id=(c, chip), device_id_type=MESH)

    def tagged(src, dst, kind, t, c, chip):
        return remote(src, dst, ssem.at[kind, t], rsem.at[kind, t], c, chip)

    def sent(region, kind, t):
        tagged(region, region, kind, t, other, lb).wait_send()

    def came(region, kind, t):
        tagged(region, region, kind, t, other, lb).wait_recv()

    def half_rows(h):
        return pl.ds(pl.multiple_of(h * EH, EH), EH)

    def rs_copy(t, h, m):
        return tagged(outb.at[t, m, half_rows(h)], rsb.at[t, h, m - 1], RS + h, t, core, rpeer(m))

    def gat_rows(m, h):
        return pl.ds(pl.multiple_of(core * half + flip(side, m) * EC + h * EH, EH), EH)

    def g_copy(t, h, m):
        reg = gat.at[t, gat_rows(0, h)]
        return tagged(reg, reg, GA + h, t, core, gpeer(m))

    def fw_copy(t, h, m):
        reg = gat.at[t, gat_rows(m, h)]
        return tagged(reg, reg, FW + h, t, other, lb)

    seven_halves = gat.at[0, pl.ds(0, 7 * EH)]
    eight_halves = gat.at[0, pl.ds(0, 8 * EH)]

    def p_copy(t, m):
        reg = pg.at[t, :, myrows, mycols]
        return tagged(reg, reg, PS, t, core, gpeer(m))

    def pf_copy(t):
        reg = pg.at[t, :, :, mycols]
        return tagged(reg, reg, PF, t, other, lb)

    seven_psi = pg.at[0, :, pl.ds(0, 7 * 16), pl.ds(0, half)]

    def f_copy(t, m):
        src = fsend.at[t, :, pl.ds(pl.multiple_of(flip(low, m) * 16, 16), 16)]
        return tagged(src, frecv.at[t, eset], FI, t, core, gpeer(m))

    seven_fin = frecv.at[0, pl.ds(0, 7)]

    def l_region(n, m, j):
        first, count = THIRDS[j]
        return ls.at[n, pl.ds(core * lhalf + first, count), pl.ds(pl.multiple_of(flip(low, m) * 16, 16), 16)]

    def l_copy(n, m, j, d):
        reg = l_region(n, m, j)
        return remote(reg, reg, ssem.at[LS, n], lsem.at[n, j, m + d], core, gpeer(d))

    def lf_copy(n, m, j):
        reg = l_region(n, m, j)
        return tagged(reg, reg, LF, n, other, lb)

    seven_l = ls.at[0, pl.ds(0, lhalf), pl.ds(0, 7 * 16)]

    group = [(c, m) for c in range(2) for m in range(8) if c or m]

    def flip_core(c):
        return core + c * (1 - 2 * core)

    def g_send(t, kind, part):
        asend[kind, t, 0] = part
        gbuf[kind, t, core * 8 + eset] = part
        for c, m in group:
            tagged(asend.at[kind, t, 0], gbuf.at[kind, t, core * 8 + eset], AG + kind, t, flip_core(c), gpeer(m)).start()

    def g_sum(t, kind):
        came(gbuf.at[kind, t, pl.ds(0, 15)], AG + kind, t)
        return sum(gbuf[kind, t, j] for j in range(16))

    def r_send(t, kind, part):
        asend[kind, t, 1] = part
        rbuf[kind, t, aset] = part
        for m in SEVEN:
            tagged(asend.at[kind, t, 1], rbuf.at[kind, t, aset], AR + kind, t, core, rpeer(m)).start()

    def r_sum(t, kind):
        came(rbuf.at[kind, t, pl.ds(0, 7)], AR + kind, t)
        return sum(rbuf[kind, t, j] for j in range(8))

    def mean(tile):
        return jnp.sum(jnp.sum(tile, axis=0, keepdims=True), axis=1, keepdims=True) / elems

    def total(t, kind):
        tile = r_sum(t, kind)
        sent(gbuf.at[kind, t, pl.ds(0, 15)], AG + kind, t)
        sent(rbuf.at[kind, t, pl.ds(0, 7)], AR + kind, t)
        return mean(tile)

    def put(t, kind, val):
        scal[kind, t] = jnp.broadcast_to(val, (8, LN))

    def get(t, kind):
        return scal[kind, t][0:1, 0:1]

    def record(kind, t, s, val):
        rows = lax.broadcasted_iota(jnp.int32, (2, STEPS), 0)
        cols = lax.broadcasted_iota(jnp.int32, (2, STEPS), 1)
        sums_out[kind] = jnp.where(jnp.logical_and(rows == t, cols == s), val, sums_out[kind])

    psi_ld = pltpu.make_async_copy(psi_ref, praw, ldsem.at[0])
    psi_ld.start()
    l_ld = pltpu.make_async_copy(left_ref, lst, ldsem.at[1])
    l_ld.start()
    r_ld = pltpu.make_async_copy(right_ref.at[:, pl.ds(pl.multiple_of(eset * EC, EC), EC)], rf, ldsem.at[2])
    r_ld.start()
    barrier = pltpu.get_barrier_semaphore()
    for c, m in group:
        pl.semaphore_signal(barrier, inc=1, device_id=(flip_core(c), gpeer(m)), device_id_type=MESH)
    for m in SEVEN:
        pl.semaphore_signal(barrier, inc=1, device_id=(core, rpeer(m)), device_id_type=MESH)
    psi_ld.wait()
    parts = []
    for t in range(2):
        acc = 0
        for ij in range(PH):
            val = praw[t, :, ij // 2, ij % 2, :]
            pg[t, ij, myrows, mycols] = val
            acc = acc + val * val
        parts.append(fold(acc))
    sums_out[...] = jnp.zeros(sums_out.shape, F32)
    pl.semaphore_wait(barrier, len(group) + len(SEVEN))
    for t in range(2):
        g_send(t, NORM, parts[t])
    for m in SEVEN:
        p_copy(0, m).start()
    l_ld.wait()

    def perm_body(l, carry):
        lane = lax.broadcasted_iota(jnp.int32, (16, LN), 1) // 32
        for hz in range(2):
            for hy in range(2):
                src = [lst[l, :, pl.ds((4 * hz + 2 * q + hy) * LN, LN)] for q in range(2)]
                for hx in range(2):
                    pick = None
                    for c in range(PH):
                        shift = (c - 2 * (c % 2) - hx) * 32 % LN
                        val = pltpu.roll(src[c // 2], shift, 1) if shift else src[c // 2]
                        pick = val if pick is None else jnp.where(lane == c, val, pick)
                    rel = [p + q * (1 - 2 * p) for p, q in zip((hz, hy, hx), high)]
                    far = sum(rel) // 2
                    rank = [p + far * (1 - 2 * p) for p in rel]
                    j = 3 - (3 * rank[0] + 2 * rank[1] + rank[2])
                    ls[1 - far, l, myrows, pl.ds(pl.multiple_of(j * LN, LN), LN)] = pick
        return carry

    lax.fori_loop(0, mpo, perm_body, 0)
    for n in range(2):
        for j in range(3):
            for d in NEAR:
                l_copy(n, 0, j, d).start()
    w0, w1, w2 = split3(wmat_ref[...])
    wpk[...] = jnp.concatenate([w0, w0, w0, w1, w1, w2], axis=1)
    for t in range(2):
        r_send(t, NORM, g_sum(t, NORM))

    def l_take(n, m, j, links):
        reg = l_region(n, m, j)
        remote(reg, reg, ssem.at[LS, n], lsem.at[n, j, m], other, lb).wait_recv()
        for d in links:
            l_copy(n, m, j, d).start()
        lf_copy(n, m, j).start()

    def l_rest(n):
        for j in range(3):
            a, b, c = ORDERS[j]
            for m in (a + c, b + c, a + b + c):
                l_take(n, m, j, ())
        came(seven_l, LF, n)

        def split_body(l, carry):
            for k, part in enumerate(split3(ls[n, l])):
                l3[k, n, l] = part
            return carry

        lax.fori_loop(0, mpo, split_body, 0)

    def l_first():
        for n in range(2):
            for j in range(3):
                a, b, c = ORDERS[j]
                l_take(n, a, j, (b, c))
                l_take(n, b, j, (c,))
                l_take(n, c, j, ())
        for n in range(2):
            for j in range(3):
                a, b, c = ORDERS[j]
                l_take(n, a + b, j, (c,))
        for m in SEVEN:
            p_copy(1, m).start()
        l_rest(0)

    def l_second():
        l_rest(1)
        for n in range(2):
            sent(seven_l, LS, n)
            sent(seven_l, LF, n)

    def ev_init(t):
        came(seven_psi, PS, t)
        pf_copy(t).start()
        rinv = 1.0 / jnp.sqrt(total(t, NORM))
        put(t, BETA, jnp.zeros((1, 1), F32))
        for slot in range(2):
            put(t, FAC + slot, jnp.ones((1, 1), F32))
        pf_copy(t).wait_recv()

        def tr_body(b, carry):
            rows = pl.ds(pl.multiple_of(b * LN, LN), LN)
            for ij in range(PH):
                vec[t, 0, rows, ij * LN:(ij + 1) * LN] = pg[t, ij, :, rows].T * rinv
            vec[t, 1, rows] = jnp.zeros((LN, WID), F32)
            return carry

        lax.fori_loop(0, bond // LN, tr_body, 0)
        sent(seven_psi, PS, t)
        pf_copy(t).wait_send()

    def ev_sum(t, s, h, more):
        came(rsb.at[t, h], RS + h, t)
        hv = outb[t, 0, half_rows(h)] + sum(rsb[t, h, m - 1] for m in SEVEN)
        gat[t, gat_rows(0, h)] = hv
        if h:
            rows = pl.ds(pl.multiple_of(own, EC), EC)
            g_send(t, ALPHA, fold(gat[t, rows] * vec[t, s % 2, rows]) * get(t, FAC + s % 2))

        @pl.when(more)
        def _():
            for m in SEVEN:
                g_copy(t, h, m).start()
            fw_copy(t, h, 0).start()

        sent(rsb.at[t, h], RS + h, t)

    def new_w(t, s, rows):
        cur, prev = s % 2, (s + 1) % 2
        return gat[t, rows] - get(t, ALPHA) * get(t, FAC + cur) * vec[t, cur, rows] - get(t, BETA) * get(t, FAC + prev) * vec[t, prev, rows]

    def ev_mid(t):
        r_send(t, ALPHA, g_sum(t, ALPHA))

    def ev_alpha(t, s):
        alpha = total(t, ALPHA)
        put(t, ALPHA, alpha)
        record(0, t, s, alpha)
        res = new_w(t, s, pl.ds(pl.multiple_of(own, EC), EC))
        g_send(t, BETA, fold(res * res))

    def ev_size(t):
        tile = g_sum(t, BETA)
        r_send(t, BETA, tile)
        put(t, SIZE, jnp.sqrt(mean(tile)))

    def ev_fwd(t, h):
        came(seven_halves, GA + h, t)
        for m in SEVEN:
            fw_copy(t, h, m).start()

    def ev_beta(t, s):
        beta = jnp.sqrt(total(t, BETA))
        put(t, BETA, beta)
        record(1, t, s, beta)
        put(t, FAC + (s + 1) % 2, get(t, SIZE) / beta)
        return beta

    def ev_vec(t, s):
        size = get(t, SIZE)
        rinv = jnp.where(size > 0, 1.0 / size, 0.0)

        def rows_of(first):
            def body(j, carry):
                rows = pl.ds(pl.multiple_of(first + j * LN, LN), LN)
                vec[t, (s + 1) % 2, rows] = new_w(t, s, rows) * rinv
                return carry

            lax.fori_loop(0, half // LN, body, 0)

        rows_of(core * half)
        for h in range(2):
            came(eight_halves, FW + h, t)
        rows_of(other * half)
        for h in range(2):
            sent(eight_halves, FW + h, t)
            sent(seven_halves, GA + h, t)

    def r_phase(t, s, h):
        xv = jnp.dot(rf[:, half_rows(h), :].reshape(mpo * EH, bond), vec[t, s % 2], preferred_element_type=F32, precision=HI)
        for r in range(mpo):
            for ij in range(PH):
                xf[pl.ds((ij * mpo + r) * NX, EH), :] = xv[r * EH:(r + 1) * EH, ij * LN:(ij + 1) * LN]

    def w_phase(t, s, h):
        fac = get(t, FAC + s % 2)
        for e in range(0, EH, 2):
            xs = jnp.concatenate([xf[pl.ds(e + q, PH * mpo, stride=NX), :] for q in range(2)], axis=1) * fac
            x0, x1, x2 = split3(xs)
            yv = jnp.dot(wpk[...], jnp.concatenate([x0, x1, x2, x0, x1, x0], axis=0), preferred_element_type=F32)
            for q in range(2):
                yf[pl.ds(h * EH + e + q, PH * mpo, stride=NY), :] = yv[:, q * LN:(q + 1) * LN]

    def l_phase(t, h, n):
        lhs = [jnp.concatenate([yf[pl.ds(pl.multiple_of((l * PH + mn) * NY + h * EH, 8), EH), :] for mn in range(PH)], axis=0) for l in range(mpo)]
        y0, y1, y2 = split3(jnp.concatenate(lhs, axis=1))
        b0, b1, b2 = [l3[k, n].reshape(mpo * LN, PH * LN) for k in range(3)]
        p0 = jnp.dot(jnp.concatenate([y0, y1, y2], axis=0), b0, preferred_element_type=F32)
        p1 = jnp.dot(jnp.concatenate([y0, y1], axis=0), b1, preferred_element_type=F32)
        p2 = jnp.dot(y0, b2, preferred_element_type=F32)
        ov = ((p0[2 * LN:] + p1[LN:]) + p2) + (p0[LN:2 * LN] + p1[:LN]) + p0[:LN]
        for j in range(PH):
            m = FAR[j] + n * (CLOSE[j] - FAR[j])
            for mn in range(PH):
                outb[t, m, half_rows(h), mn * LN:(mn + 1) * LN] = ov[mn * EH:(mn + 1) * EH, j * LN:(j + 1) * LN]

    def step_body(it, carry):
        t, s = it % 2, it // 2
        ot = 1 - t
        os = (it + 1) // 2 - 1
        first = 1 - (it + 2 * STEPS - 1) // (2 * STEPS)
        has = it >= 1
        more = jnp.logical_and(has, it < 2 * STEPS - 1)

        @pl.when(it < 2)
        def _():
            ev_init(t)

        @pl.when(it >= 2)
        def _():
            ev_vec(t, s - 1)

        @pl.when(has)
        def _():
            ev_sum(ot, os, 0, more)

        @pl.when(it == 0)
        def _():
            r_ld.wait()

        def slot_body(q, c2):
            h = first * (q % 2) + (1 - first) * (q // 3)
            n = first * ((q - 2) // 2) + (1 - first) * (q % 3 - 1)
            is_rw = jnp.logical_or(jnp.logical_and(it == 0, q < 2), jnp.logical_and(has, q % 3 == 0))

            def at(cond, slot, event, *args):
                @pl.when(jnp.logical_and(cond, q == slot))
                def _():
                    event(*args)

            @pl.when(is_rw)
            def _():
                r_phase(t, s, h)
                at(has, 0, ev_sum, ot, os, 1, more)
                at(it >= 2, 0, ev_beta, t, s - 1)
                at(has, 3, ev_alpha, ot, os)
                at(more, 3, ev_fwd, ot, 1)
                w_phase(t, s, h)

            @pl.when(jnp.logical_not(is_rw))
            def _():
                at(it == 0, 2, l_first)
                at(it == 0, 4, l_second)
                l_phase(t, h, n)
                at(has, 1, ev_mid, ot)
                at(more, 2, ev_fwd, ot, 0)
                at(has, 4, ev_size, ot)

                @pl.when(n == 0)
                def _():
                    for m in FAR:
                        rs_copy(t, h, m).start()

                @pl.when(n == 1)
                def _():
                    for m in NEAR:
                        rs_copy(t, h, m).start()

            return c2

        lax.fori_loop(0, 6, slot_body, 0)
        return carry

    lax.fori_loop(0, 2 * STEPS, step_body, 0)

    last = STEPS - 1

    def finish(t):
        beta = ev_beta(t, last)
        res = new_last[t] * (1.0 / beta)
        for q in range(2):
            pair = [res[:, j * LN:(j + 1) * LN] for j in (2 * q, 2 * q + 1)]
            fsend[t, q] = jnp.concatenate(pair, axis=0).T
        for m in SEVEN:
            f_copy(t, m).start()
        frecv[t, eset] = fsend[t, :, myrows]

    def assemble(t):
        came(seven_fin, FI, t)
        for i in range(2):
            for j in range(2):
                psi_out[t, :, i, j, :] = jnp.concatenate([frecv[t, g, i][:, j * EC:(j + 1) * EC] for g in range(8)], axis=1)
        sent(seven_fin, FI, t)

    ownrows = pl.ds(pl.multiple_of(own, EC), EC)
    new_last = {}
    ev_sum(1, last, 0, False)
    ev_sum(1, last, 1, False)
    new_last[0] = new_w(0, last, ownrows)
    finish(0)
    ev_mid(1)
    assemble(0)
    ev_alpha(1, last)
    new_last[1] = new_w(1, last, ownrows)
    ev_size(1)
    finish(1)
    assemble(1)


def solution(mesh):
    psi_spec = P(None, "lb", None, None, "rb")

    def local_run(psi_loc, left_loc, right_loc, mpo_pair):
        rows = psi_loc.shape[1]
        mpo, bond = left_loc.shape[1:]
        left_t = jnp.transpose(left_loc, (1, 0, 2))
        right_t = jnp.transpose(right_loc, (1, 0, 2))
        wmat = jnp.transpose(mpo_pair.reshape(mpo, mpo, PH, PH), (0, 3, 2, 1)).reshape(PH * mpo, PH * mpo)
        dma = pltpu.SemaphoreType.DMA
        any_spec = pl.BlockSpec(memory_space=pl.ANY)
        vm = pl.BlockSpec(memory_space=pltpu.VMEM)
        f32_shapes = [
            (mpo, EC, bond),
            (2, mpo, LN, WID),
            (mpo, rows, bond),
            (2, bond, WID),
            (2, 2, bond, WID),
            (2, PH, LN, bond),
            psi_loc.shape,
            (PH * mpo * NX, LN),
            (PH * mpo * NY, LN),
            (2, 8, EC, WID),
            (2, 2, 7, EH, WID),
        ]
        small = [(3, 2, 16, 8, LN), (3, 2, 8, 8, LN), (3, 2, 2, 8, LN), (SIZE + 1, 2, 8, LN), (2, 2, LN, LN), (2, 8, 2, 16, LN)]
        call = pl.pallas_call(
            functools.partial(kernel, (bond, mpo, float(bond * bond * PH))),
            out_shape=[jax.ShapeDtypeStruct(shape, F32) for shape in (psi_loc.shape, (2, 2, STEPS))],
            in_specs=[any_spec, any_spec, any_spec, vm],
            out_specs=[vm] * 2,
            scratch_shapes=[pltpu.VMEM(shape, F32) for shape in f32_shapes]
            + [pltpu.VMEM((3, 2, mpo, LN, WID), BF16), pltpu.VMEM((PH * mpo, 6 * PH * mpo), BF16)]
            + [pltpu.VMEM(shape, F32) for shape in small]
            + [dma((KINDS, 2))] * 2
            + [dma((2, 3, 8)), dma((3,))],
            compiler_params=pltpu.CompilerParams(vmem_limit_bytes=63 << 20, has_side_effects=True, collective_id=0),
            name="lanczos",
        )
        psi_next, sums = call(psi_loc, left_t, right_t, wmat)
        return sums[0], sums[1], psi_next

    return jax.shard_map(local_run, mesh=mesh, in_specs=(psi_spec, P("lb", None, None), P("rb", None, None), P()), out_specs=(P(), P(), psi_spec), check_vma=False)
```

time: 346 us -> 284 us (0.82)
  Pallas kernels: 339 us -> 278 us
    pallas_call x1, Pallas kernels: 339 us -> 278 us  [local_run(): psi_next, sums = call(psi_loc, left_t, right_t, wmat)]
where the time goes in v2:
time: 284 us; the launch traced here: 283 us
  Pallas kernels  278 us (98%)
  local copies, waits for them, and re-layouts  4.63 us (2%)
    pallas_call x1, Pallas kernels, local_run(): psi_next, sums = call(psi_loc, left_t, right_t, wmat)  278 us

profile of v2, /device:TPU:1, one launch (start us, length us, event | category | flops | bytes accessed | tf_op | source)
XLA Modules:
  0.0 283.1 jit_solution(3116421415395049236)
XLA Ops:
  0.6 1.0 copy.9
  1.6 0.7 reshape.13.wmat_ref
  2.3 277.9 %lanczos.1 = (f32[2,16,2,2,512]{4,3,2,1,0:T(2,128)}, f32[2,2,4]{2,1,0:T(2,128)}) custom-call(f32[2,16,2,2,512]{4,3,2,1,0:T(2,128)} %psi_ref.1, f32[20,16,1024]{2,1,0:T(8,128)} %bitcast.11, f32[20,512,1024]{2,1,0:T(8,128)} %bitcast.10, f32[80,80]{1,0:T(8,128)} %reshape.13.wmat_ref), custom_call_target="tpu_custom_call" | custom-call | tf_op jit(solution)/shard_map/lanczos/pallas_call | solution.py:547
  280.2 1.3 slice_bitcast_fusion
  281.5 1.7 copy.11

commit v3 on v2

--- a/solution.py
+++ b/solution.py
@@ -22,14 +22,14 @@
 FAR = (3, 5, 6, 7)
 CLOSE = (4, 2, 1, 0)
 NEAR = CLOSE[:3]
-SEVEN = FAR + NEAR
+SEVEN = FAR[::-1] + NEAR
 ALPHA, BETA, NORM, FAC = range(4)
 SIZE = FAC + 2
 RS, GA, FW = 0, 2, 4
 PS, PF, FI, AG = range(6, 10)
 AR = AG + 3
 LS, LF = AR + 3, AR + 4
-KINDS = AR + 5
+KINDS = AR + 6
 THIRDS = ((0, 4), (4, 3), (7, 3))
 ORDERS = ((4, 2, 1), (2, 1, 4), (1, 4, 2))
 
@@ -140,9 +140,10 @@
 
     def lf_copy(n, m, j):
         reg = l_region(n, m, j)
-        return tagged(reg, reg, LF, n, other, lb)
+        return tagged(reg, reg, LF + (m in FAR), n, other, lb)
 
     seven_l = ls.at[0, pl.ds(0, lhalf), pl.ds(0, 7 * 16)]
+    near_l, far_l = [ls.at[0, pl.ds(0, lhalf), pl.ds(0, len(part) * 16)] for part in (NEAR, FAR)]
 
     group = [(c, m) for c in range(2) for m in range(8) if c or m]
 
@@ -252,19 +253,23 @@
             l_copy(n, m, j, d).start()
         lf_copy(n, m, j).start()
 
+    def split_rows(n, offsets):
+        def split_body(l, carry):
+            for m in offsets:
+                rows = pl.ds(pl.multiple_of(flip(low, m) * 16, 16), 16)
+                for k, part in enumerate(split3(ls[n, l, rows])):
+                    l3[k, n, l, rows] = part
+            return carry
+
+        lax.fori_loop(0, mpo, split_body, 0)
+
     def l_rest(n):
         for j in range(3):
             a, b, c = ORDERS[j]
             for m in (a + c, b + c, a + b + c):
                 l_take(n, m, j, ())
-        came(seven_l, LF, n)
-
-        def split_body(l, carry):
-            for k, part in enumerate(split3(ls[n, l])):
-                l3[k, n, l] = part
-            return carry
-
-        lax.fori_loop(0, mpo, split_body, 0)
+        came(far_l, LF + 1, n)
+        split_rows(n, FAR)
 
     def l_first():
         for n in range(2):
@@ -274,6 +279,9 @@
                 l_take(n, b, j, (c,))
                 l_take(n, c, j, ())
         for n in range(2):
+            came(near_l, LF, n)
+            split_rows(n, CLOSE)
+        for n in range(2):
             for j in range(3):
                 a, b, c = ORDERS[j]
                 l_take(n, a + b, j, (c,))
@@ -285,25 +293,32 @@
         l_rest(1)
         for n in range(2):
             sent(seven_l, LS, n)
-            sent(seven_l, LF, n)
-
-    def ev_init(t):
+            sent(near_l, LF, n)
+            sent(far_l, LF + 1, n)
+
+    def psi_pass(t):
         came(seven_psi, PS, t)
         pf_copy(t).start()
+
+    def ev_init(t):
         rinv = 1.0 / jnp.sqrt(total(t, NORM))
         put(t, BETA, jnp.zeros((1, 1), F32))
         for slot in range(2):
             put(t, FAC + slot, jnp.ones((1, 1), F32))
+
+        def turn(first):
+            def tr_body(b, carry):
+                rows = pl.ds(pl.multiple_of(first + b * LN, LN), LN)
+                for ij in range(PH):
+                    vec[t, 0, rows, ij * LN:(ij + 1) * LN] = pg[t, ij, :, rows].T * rinv
+                vec[t, 1, rows] = jnp.zeros((LN, WID), F32)
+                return carry
+
+            lax.fori_loop(0, half // LN, tr_body, 0)
+
+        turn(core * half)
         pf_copy(t).wait_recv()
-
-        def tr_body(b, carry):
-            rows = pl.ds(pl.multiple_of(b * LN, LN), LN)
-            for ij in range(PH):
-                vec[t, 0, rows, ij * LN:(ij + 1) * LN] = pg[t, ij, :, rows].T * rinv
-            vec[t, 1, rows] = jnp.zeros((LN, WID), F32)
-            return carry
-
-        lax.fori_loop(0, bond // LN, tr_body, 0)
+        turn(other * half)
         sent(seven_psi, PS, t)
         pf_copy(t).wait_send()
 
@@ -337,6 +352,15 @@
         res = new_w(t, s, pl.ds(pl.multiple_of(own, EC), EC))
         g_send(t, BETA, fold(res * res))
 
+        @pl.when(s == STEPS - 1)
+        def _():
+            for q in range(2):
+                pair = [res[:, j * LN:(j + 1) * LN] for j in (2 * q, 2 * q + 1)]
+                fsend[t, q] = jnp.concatenate(pair, axis=0).T
+            for m in SEVEN:
+                f_copy(t, m).start()
+            frecv[t, eset] = fsend[t, :, myrows]
+
     def ev_size(t):
         tile = g_sum(t, BETA)
         r_send(t, BETA, tile)
@@ -374,29 +398,30 @@
             sent(eight_halves, FW + h, t)
             sent(seven_halves, GA + h, t)
 
-    def r_phase(t, s, h):
-        xv = jnp.dot(rf[:, half_rows(h), :].reshape(mpo * EH, bond), vec[t, s % 2], preferred_element_type=F32, precision=HI)
+    def r_phase(t, s, first, count):
+        rows = rf[:, pl.ds(pl.multiple_of(first, 16), count), :].reshape(mpo * count, bond)
+        xv = jnp.dot(rows, vec[t, s % 2], preferred_element_type=F32, precision=HI)
+        base = first % EH
         for r in range(mpo):
             for ij in range(PH):
-                xf[pl.ds((ij * mpo + r) * NX, EH), :] = xv[r * EH:(r + 1) * EH, ij * LN:(ij + 1) * LN]
-
-    def w_phase(t, s, h):
-        fac = get(t, FAC + s % 2)
+                xf[pl.ds(pl.multiple_of((ij * mpo + r) * NX + base, 8), count), :] = xv[r * count:(r + 1) * count, ij * LN:(ij + 1) * LN]
+
+    def w_phase(h):
         for e in range(0, EH, 2):
-            xs = jnp.concatenate([xf[pl.ds(e + q, PH * mpo, stride=NX), :] for q in range(2)], axis=1) * fac
+            xs = jnp.concatenate([xf[pl.ds(e + q, PH * mpo, stride=NX), :] for q in range(2)], axis=1)
             x0, x1, x2 = split3(xs)
             yv = jnp.dot(wpk[...], jnp.concatenate([x0, x1, x2, x0, x1, x0], axis=0), preferred_element_type=F32)
             for q in range(2):
                 yf[pl.ds(h * EH + e + q, PH * mpo, stride=NY), :] = yv[:, q * LN:(q + 1) * LN]
 
-    def l_phase(t, h, n):
+    def l_phase(t, s, h, n):
         lhs = [jnp.concatenate([yf[pl.ds(pl.multiple_of((l * PH + mn) * NY + h * EH, 8), EH), :] for mn in range(PH)], axis=0) for l in range(mpo)]
         y0, y1, y2 = split3(jnp.concatenate(lhs, axis=1))
         b0, b1, b2 = [l3[k, n].reshape(mpo * LN, PH * LN) for k in range(3)]
         p0 = jnp.dot(jnp.concatenate([y0, y1, y2], axis=0), b0, preferred_element_type=F32)
         p1 = jnp.dot(jnp.concatenate([y0, y1], axis=0), b1, preferred_element_type=F32)
         p2 = jnp.dot(y0, b2, preferred_element_type=F32)
-        ov = ((p0[2 * LN:] + p1[LN:]) + p2) + (p0[LN:2 * LN] + p1[:LN]) + p0[:LN]
+        ov = (((p0[2 * LN:] + p1[LN:]) + p2) + (p0[LN:2 * LN] + p1[:LN]) + p0[:LN]) * get(t, FAC + s % 2)
         for j in range(PH):
             m = FAR[j] + n * (CLOSE[j] - FAR[j])
             for mn in range(PH):
@@ -438,25 +463,41 @@
 
             @pl.when(is_rw)
             def _():
-                r_phase(t, s, h)
-                at(has, 0, ev_sum, ot, os, 1, more)
+                @pl.when(h == 0)
+                def _():
+                    r_phase(t, s, 0, EH)
+
+                @pl.when(h == 1)
+                def _():
+                    def part(k, c3):
+                        r_phase(t, s, EH + k * (EH // 2), EH // 2)
+
+                        @pl.when(jnp.logical_and(has, k == 0))
+                        def _():
+                            ev_mid(ot)
+
+                        return c3
+
+                    lax.fori_loop(0, 2, part, 0)
+
+                w_phase(h)
                 at(it >= 2, 0, ev_beta, t, s - 1)
                 at(has, 3, ev_alpha, ot, os)
-                at(more, 3, ev_fwd, ot, 1)
-                w_phase(t, s, h)
 
             @pl.when(jnp.logical_not(is_rw))
             def _():
                 at(it == 0, 2, l_first)
                 at(it == 0, 4, l_second)
-                l_phase(t, h, n)
-                at(has, 1, ev_mid, ot)
+                l_phase(t, s, h, n)
+                at(it == 0, 4, psi_pass, 1)
+                at(has, 1, ev_sum, ot, os, 1, more)
                 at(more, 2, ev_fwd, ot, 0)
-                at(has, 4, ev_size, ot)
+                at(more, 4, ev_fwd, ot, 1)
+                at(has, 5, ev_size, ot)
 
                 @pl.when(n == 0)
                 def _():
-                    for m in FAR:
+                    for m in FAR[::-1]:
                         rs_copy(t, h, m).start()
 
                 @pl.when(n == 1)
@@ -469,40 +510,26 @@
         lax.fori_loop(0, 6, slot_body, 0)
         return carry
 
+    psi_pass(0)
     lax.fori_loop(0, 2 * STEPS, step_body, 0)
 
     last = STEPS - 1
 
     def finish(t):
-        beta = ev_beta(t, last)
-        res = new_last[t] * (1.0 / beta)
-        for q in range(2):
-            pair = [res[:, j * LN:(j + 1) * LN] for j in (2 * q, 2 * q + 1)]
-            fsend[t, q] = jnp.concatenate(pair, axis=0).T
-        for m in SEVEN:
-            f_copy(t, m).start()
-        frecv[t, eset] = fsend[t, :, myrows]
-
-    def assemble(t):
+        rinv = 1.0 / ev_beta(t, last)
         came(seven_fin, FI, t)
         for i in range(2):
             for j in range(2):
-                psi_out[t, :, i, j, :] = jnp.concatenate([frecv[t, g, i][:, j * EC:(j + 1) * EC] for g in range(8)], axis=1)
+                psi_out[t, :, i, j, :] = jnp.concatenate([frecv[t, g, i][:, j * EC:(j + 1) * EC] for g in range(8)], axis=1) * rinv
         sent(seven_fin, FI, t)
 
-    ownrows = pl.ds(pl.multiple_of(own, EC), EC)
-    new_last = {}
     ev_sum(1, last, 0, False)
     ev_sum(1, last, 1, False)
-    new_last[0] = new_w(0, last, ownrows)
     finish(0)
     ev_mid(1)
-    assemble(0)
     ev_alpha(1, last)
-    new_last[1] = new_w(1, last, ownrows)
     ev_size(1)
     finish(1)
-    assemble(1)
 
 
 def solution(mesh):

time: 284 us -> 281 us (0.989)
  Pallas kernels: 278 us -> 275 us
where the time goes in v3:
time: 281 us; the launch traced here: 280 us
  Pallas kernels  275 us (98%)
  local copies, waits for them, and re-layouts  4.63 us (2%)
    pallas_call x1, Pallas kernels, local_run(): psi_next, sums = call(psi_loc, left_t, right_t, wmat)  275 us

profile of v3, /device:TPU:1, one launch (start us, length us, event | category | flops | bytes accessed | tf_op | source)
XLA Modules:
  0.0 280.4 jit_solution(4640885384719342351)
XLA Ops:
  0.6 1.0 copy.9
  1.6 0.7 reshape.13.wmat_ref
  2.3 275.1 %lanczos.1 = (f32[2,16,2,2,512]{4,3,2,1,0:T(2,128)}, f32[2,2,4]{2,1,0:T(2,128)}) custom-call(f32[2,16,2,2,512]{4,3,2,1,0:T(2,128)} %psi_ref.1, f32[20,16,1024]{2,1,0:T(8,128)} %bitcast.11, f32[20,512,1024]{2,1,0:T(8,128)} %bitcast.10, f32[80,80]{1,0:T(8,128)} %reshape.13.wmat_ref), custom_call_target="tpu_custom_call" | custom-call | tf_op jit(solution)/shard_map/lanczos/pallas_call | solution.py:574
  277.5 1.3 slice_bitcast_fusion
  278.7 1.7 copy.11

commit v4 on v3

--- a/solution.py
+++ b/solution.py
@@ -47,6 +47,11 @@
     return sum(acc[j:j + 8] for j in range(0, val.shape[0], 8))
 
 
+def fold_max(val):
+    acc = functools.reduce(jnp.maximum, [val[:, j:j + LN] for j in range(0, val.shape[1], LN)])
+    return functools.reduce(jnp.maximum, [acc[j:j + 8] for j in range(0, val.shape[0], 8)])
+
+
 def bits(m):
     return m // 4, (m // 2) % 2, m % 2
 
@@ -150,21 +155,26 @@
     def flip_core(c):
         return core + c * (1 - 2 * core)
 
-    def g_send(t, kind, part):
-        asend[kind, t, 0] = part
-        gbuf[kind, t, core * 8 + eset] = part
+    def g_send(t, kind, *parts):
+        tiles = pl.ds(0, len(parts))
+        for k, part in enumerate(parts):
+            asend[kind, t, 0, k] = part
+            gbuf[kind, t, core * 8 + eset, k] = part
         for c, m in group:
-            tagged(asend.at[kind, t, 0], gbuf.at[kind, t, core * 8 + eset], AG + kind, t, flip_core(c), gpeer(m)).start()
+            tagged(asend.at[kind, t, 0, tiles], gbuf.at[kind, t, core * 8 + eset, tiles], AG + kind, t, flip_core(c), gpeer(m)).start()
+
+    def g_bytes(t, kind):
+        return gbuf.at[kind, t, pl.ds(0, 15), pl.ds(0, 2 if kind == ALPHA else 1)]
 
     def g_sum(t, kind):
-        came(gbuf.at[kind, t, pl.ds(0, 15)], AG + kind, t)
-        return sum(gbuf[kind, t, j] for j in range(16))
+        came(g_bytes(t, kind), AG + kind, t)
+        return sum(gbuf[kind, t, j, 0] for j in range(16))
 
     def r_send(t, kind, part):
-        asend[kind, t, 1] = part
+        asend[kind, t, 1, 0] = part
         rbuf[kind, t, aset] = part
         for m in SEVEN:
-            tagged(asend.at[kind, t, 1], rbuf.at[kind, t, aset], AR + kind, t, core, rpeer(m)).start()
+            tagged(asend.at[kind, t, 1, 0], rbuf.at[kind, t, aset], AR + kind, t, core, rpeer(m)).start()
 
     def r_sum(t, kind):
         came(rbuf.at[kind, t, pl.ds(0, 7)], AR + kind, t)
@@ -175,7 +185,7 @@
 
     def total(t, kind):
         tile = r_sum(t, kind)
-        sent(gbuf.at[kind, t, pl.ds(0, 15)], AG + kind, t)
+        sent(g_bytes(t, kind), AG + kind, t)
         sent(rbuf.at[kind, t, pl.ds(0, 7)], AR + kind, t)
         return mean(tile)
 
@@ -271,13 +281,14 @@
         came(far_l, LF + 1, n)
         split_rows(n, FAR)
 
+    def l_near(n):
+        for j in range(3):
+            a, b, c = ORDERS[j]
+            l_take(n, a, j, (b, c))
+            l_take(n, b, j, (c,))
+            l_take(n, c, j, ())
+
     def l_first():
-        for n in range(2):
-            for j in range(3):
-                a, b, c = ORDERS[j]
-                l_take(n, a, j, (b, c))
-                l_take(n, b, j, (c,))
-                l_take(n, c, j, ())
         for n in range(2):
             came(near_l, LF, n)
             split_rows(n, CLOSE)
@@ -328,7 +339,8 @@
         gat[t, gat_rows(0, h)] = hv
         if h:
             rows = pl.ds(pl.multiple_of(own, EC), EC)
-            g_send(t, ALPHA, fold(gat[t, rows] * vec[t, s % 2, rows]) * get(t, FAC + s % 2))
+            hv = gat[t, rows]
+            g_send(t, ALPHA, fold(hv * vec[t, s % 2, rows]) * get(t, FAC + s % 2), fold_max(jnp.abs(hv)))
 
         @pl.when(more)
         def _():
@@ -344,10 +356,13 @@
 
     def ev_mid(t):
         r_send(t, ALPHA, g_sum(t, ALPHA))
+        tile = functools.reduce(jnp.maximum, [gbuf[ALPHA, t, j, 1] for j in range(16)])
+        put(t, SIZE, jnp.max(jnp.max(tile, axis=0, keepdims=True), axis=1, keepdims=True))
 
     def ev_alpha(t, s):
         alpha = total(t, ALPHA)
         put(t, ALPHA, alpha)
+        put(t, SIZE, jnp.maximum(get(t, SIZE), jnp.maximum(jnp.abs(alpha), get(t, BETA))))
         record(0, t, s, alpha)
         res = new_w(t, s, pl.ds(pl.multiple_of(own, EC), EC))
         g_send(t, BETA, fold(res * res))
@@ -361,10 +376,8 @@
                 f_copy(t, m).start()
             frecv[t, eset] = fsend[t, :, myrows]
 
-    def ev_size(t):
-        tile = g_sum(t, BETA)
-        r_send(t, BETA, tile)
-        put(t, SIZE, jnp.sqrt(mean(tile)))
+    def ev_pass(t):
+        r_send(t, BETA, g_sum(t, BETA))
 
     def ev_fwd(t, h):
         came(seven_halves, GA + h, t)
@@ -377,6 +390,12 @@
         record(1, t, s, beta)
         put(t, FAC + (s + 1) % 2, get(t, SIZE) / beta)
         return beta
+
+    def ev_scale(t, s):
+        ev_beta(t, s - 1)
+        fac = get(t, FAC + s % 2)
+        for m in range(8):
+            outb[t, m, half_rows(0)] = outb[t, m, half_rows(0)] * fac
 
     def ev_vec(t, s):
         size = get(t, SIZE)
@@ -421,7 +440,7 @@
         p0 = jnp.dot(jnp.concatenate([y0, y1, y2], axis=0), b0, preferred_element_type=F32)
         p1 = jnp.dot(jnp.concatenate([y0, y1], axis=0), b1, preferred_element_type=F32)
         p2 = jnp.dot(y0, b2, preferred_element_type=F32)
-        ov = (((p0[2 * LN:] + p1[LN:]) + p2) + (p0[LN:2 * LN] + p1[:LN]) + p0[:LN]) * get(t, FAC + s % 2)
+        ov = (((p0[2 * LN:] + p1[LN:]) + p2) + (p0[LN:2 * LN] + p1[:LN]) + p0[:LN]) * jnp.where(h == 1, get(t, FAC + s % 2), 1.0)
         for j in range(PH):
             m = FAR[j] + n * (CLOSE[j] - FAR[j])
             for mn in range(PH):
@@ -443,13 +462,13 @@
         def _():
             ev_vec(t, s - 1)
 
-        @pl.when(has)
-        def _():
-            ev_sum(ot, os, 0, more)
-
         @pl.when(it == 0)
         def _():
             r_ld.wait()
+
+        def send_part(h, part):
+            for m in part:
+                rs_copy(t, h, m).start()
 
         def slot_body(q, c2):
             h = first * (q % 2) + (1 - first) * (q // 3)
@@ -463,26 +482,24 @@
 
             @pl.when(is_rw)
             def _():
-                @pl.when(h == 0)
-                def _():
-                    r_phase(t, s, 0, EH)
-
-                @pl.when(h == 1)
-                def _():
-                    def part(k, c3):
-                        r_phase(t, s, EH + k * (EH // 2), EH // 2)
-
-                        @pl.when(jnp.logical_and(has, k == 0))
-                        def _():
-                            ev_mid(ot)
-
-                        return c3
-
-                    lax.fori_loop(0, 2, part, 0)
-
+                def part(k, c3):
+                    r_phase(t, s, h * EH + k * (EH // 2), EH // 2)
+
+                    @pl.when(k == 0)
+                    def _():
+                        at(it == 0, 1, l_near, 1)
+                        at(it >= 2, 0, ev_pass, t)
+                        at(has, 0, ev_sum, ot, os, 0, more)
+                        at(has, 3, ev_mid, ot)
+                        at(it >= 2, 3, ev_scale, t, s)
+                        at(has, 3, send_part, 0, SEVEN)
+
+                    return c3
+
+                lax.fori_loop(0, 2, part, 0)
                 w_phase(h)
-                at(it >= 2, 0, ev_beta, t, s - 1)
-                at(has, 3, ev_alpha, ot, os)
+                at(it == 0, 0, l_near, 0)
+                at(more, 3, ev_fwd, ot, 0)
 
             @pl.when(jnp.logical_not(is_rw))
             def _():
@@ -490,20 +507,13 @@
                 at(it == 0, 4, l_second)
                 l_phase(t, s, h, n)
                 at(it == 0, 4, psi_pass, 1)
+                at(it == 0, 4, send_part, 0, SEVEN)
                 at(has, 1, ev_sum, ot, os, 1, more)
-                at(more, 2, ev_fwd, ot, 0)
+                at(has, 4, ev_alpha, ot, os)
                 at(more, 4, ev_fwd, ot, 1)
-                at(has, 5, ev_size, ot)
-
-                @pl.when(n == 0)
-                def _():
-                    for m in FAR[::-1]:
-                        rs_copy(t, h, m).start()
-
-                @pl.when(n == 1)
-                def _():
-                    for m in NEAR:
-                        rs_copy(t, h, m).start()
+                at(has, 4, send_part, 1, FAR[::-1])
+                at(it == 0, 5, send_part, 1, FAR[::-1])
+                at(it >= 0, 5, send_part, 1, NEAR)
 
             return c2
 
@@ -523,12 +533,13 @@
                 psi_out[t, :, i, j, :] = jnp.concatenate([frecv[t, g, i][:, j * EC:(j + 1) * EC] for g in range(8)], axis=1) * rinv
         sent(seven_fin, FI, t)
 
+    ev_pass(0)
     ev_sum(1, last, 0, False)
     ev_sum(1, last, 1, False)
     finish(0)
     ev_mid(1)
     ev_alpha(1, last)
-    ev_size(1)
+    ev_pass(1)
     finish(1)
 
 
@@ -557,7 +568,7 @@
             (2, 8, EC, WID),
             (2, 2, 7, EH, WID),
         ]
-        small = [(3, 2, 16, 8, LN), (3, 2, 8, 8, LN), (3, 2, 2, 8, LN), (SIZE + 1, 2, 8, LN), (2, 2, LN, LN), (2, 8, 2, 16, LN)]
+        small = [(3, 2, 16, 2, 8, LN), (3, 2, 8, 8, LN), (3, 2, 2, 2, 8, LN), (SIZE + 1, 2, 8, LN), (2, 2, LN, LN), (2, 8, 2, 16, LN)]
         call = pl.pallas_call(
             functools.partial(kernel, (bond, mpo, float(bond * bond * PH))),
             out_shape=[jax.ShapeDtypeStruct(shape, F32) for shape in (psi_loc.shape, (2, 2, STEPS))],

time: 281 us -> 273 us (0.972)
  Pallas kernels: 275 us -> 268 us
    pallas_call x1, Pallas kernels: 275 us -> 268 us  [local_run(): psi_next, sums = call(psi_loc, left_t, right_t, wmat)]
where the time goes in v4:
time: 273 us
  Pallas kernels  268 us (98%)
  local copies, waits for them, and re-layouts  4.63 us (2%)
    pallas_call x1, Pallas kernels, local_run(): psi_next, sums = call(psi_loc, left_t, right_t, wmat)  268 us

profile of v4, /device:TPU:1, one launch (start us, length us, event | category | flops | bytes accessed | tf_op | source)
XLA Modules:
  0.0 273.0 jit_solution(7843275050945481622)
XLA Ops:
  0.6 1.0 copy.9
  1.6 0.7 reshape.13.wmat_ref
  2.3 267.8 %lanczos.1 = (f32[2,16,2,2,512]{4,3,2,1,0:T(2,128)}, f32[2,2,4]{2,1,0:T(2,128)}) custom-call(f32[2,16,2,2,512]{4,3,2,1,0:T(2,128)} %psi_ref.1, f32[20,16,1024]{2,1,0:T(8,128)} %bitcast.11, f32[20,512,1024]{2,1,0:T(8,128)} %bitcast.10, f32[80,80]{1,0:T(8,128)} %reshape.13.wmat_ref), custom_call_target="tpu_custom_call" | custom-call | tf_op jit(solution)/shard_map/lanczos/pallas_call | solution.py:585
  270.1 1.3 slice_bitcast_fusion
  271.4 1.7 copy.11

commit v5 on v4

--- a/solution.py
+++ b/solution.py
@@ -31,6 +31,7 @@
 LS, LF = AR + 3, AR + 4
 KINDS = AR + 6
 THIRDS = ((0, 4), (4, 3), (7, 3))
+PLANES = ((0, 2), (2, 1), (3, 1))
 ORDERS = ((4, 2, 1), (2, 1, 4), (1, 4, 2))
 
 
@@ -42,14 +43,10 @@
     return top, mid, low
 
 
-def fold(val):
-    acc = sum(val[:, j:j + LN] for j in range(0, val.shape[1], LN))
-    return sum(acc[j:j + 8] for j in range(0, val.shape[0], 8))
-
-
-def fold_max(val):
-    acc = functools.reduce(jnp.maximum, [val[:, j:j + LN] for j in range(0, val.shape[1], LN)])
-    return functools.reduce(jnp.maximum, [acc[j:j + 8] for j in range(0, val.shape[0], 8)])
+def fold(val, op=jnp.add):
+    acc = functools.reduce(op, [val[:, j:j + LN] for j in range(0, val.shape[1], LN)])
+    acc = functools.reduce(op, [acc[j:j + 8] for j in range(0, val.shape[0], 8)])
+    return (jnp.max if op is jnp.maximum else jnp.sum)(acc, axis=0, keepdims=True)
 
 
 def bits(m):
@@ -70,7 +67,7 @@
 
 
 def kernel(cfg, psi_ref, left_ref, right_ref, wmat_ref, psi_out, sums_out,
-           rf, ls, lst, gat, vec, pg, praw, xf, yf, outb, rsb, l3, wpk, gbuf, rbuf, asend, scal, fsend, frecv, ssem, rsem, lsem, ldsem):
+           rf, ls, lst, gat, vec, pg, praw, xf, yf, outb, rsb, l3, wpk, gbuf, rbuf, asend, scal, fsend, frecv, ssem, rsem, lsem, psem, ldsem):
     bond, mpo, elems = cfg
     core, lb = lax.axis_index("rb"), lax.axis_index("lb")
     place, low, high, side = places(lb)
@@ -100,7 +97,7 @@
         tagged(region, region, kind, t, other, lb).wait_recv()
 
     def half_rows(h):
-        return pl.ds(pl.multiple_of(h * EH, EH), EH)
+        return pl.ds(h * EH, EH)
 
     def rs_copy(t, h, m):
         return tagged(outb.at[t, m, half_rows(h)], rsb.at[t, h, m - 1], RS + h, t, core, rpeer(m))
@@ -119,9 +116,41 @@
     seven_halves = gat.at[0, pl.ds(0, 7 * EH)]
     eight_halves = gat.at[0, pl.ds(0, 8 * EH)]
 
-    def p_copy(t, m):
-        reg = pg.at[t, :, myrows, mycols]
-        return tagged(reg, reg, PS, t, core, gpeer(m))
+    def p_region(t, m, j):
+        return pg.at[t, pl.ds(*PLANES[j]), pl.ds(pl.multiple_of(flip(low, m) * 16, 16), 16), mycols]
+
+    def p_copy(t, m, j, d):
+        reg = p_region(t, m, j)
+        return remote(reg, reg, ssem.at[PS, t], psem.at[t, j, m + d], core, gpeer(d))
+
+    def p_take(t, m, j, links):
+        reg = p_region(t, m, j)
+        remote(reg, reg, ssem.at[PS, t], psem.at[t, j, m], core, lb).wait_recv()
+        for d in links:
+            p_copy(t, m, j, d).start()
+
+    def p_send(t):
+        for j in range(3):
+            for d in NEAR:
+                p_copy(t, 0, j, d).start()
+
+    def p_near(t):
+        for j in range(3):
+            a, b, c = ORDERS[j]
+            p_take(t, a, j, (b, c))
+            p_take(t, b, j, (c,))
+
+    def p_last(t):
+        for j in range(3):
+            a, b, c = ORDERS[j]
+            p_take(t, a + b, j, (c,))
+
+    def p_rest(t):
+        for j in range(3):
+            a, b, c = ORDERS[j]
+            for m in (c, a + c, b + c, a + b + c):
+                p_take(t, m, j, ())
+        pf_copy(t).start()
 
     def pf_copy(t):
         reg = pg.at[t, :, :, mycols]
@@ -143,6 +172,11 @@
         reg = l_region(n, m, j)
         return remote(reg, reg, ssem.at[LS, n], lsem.at[n, j, m + d], core, gpeer(d))
 
+    def l_send(shares):
+        for n, j in shares:
+            for d in NEAR:
+                l_copy(n, 0, j, d).start()
+
     def lf_copy(n, m, j):
         reg = l_region(n, m, j)
         return tagged(reg, reg, LF + (m in FAR), n, other, lb)
@@ -155,45 +189,45 @@
     def flip_core(c):
         return core + c * (1 - 2 * core)
 
-    def g_send(t, kind, *parts):
-        tiles = pl.ds(0, len(parts))
-        for k, part in enumerate(parts):
-            asend[kind, t, 0, k] = part
-            gbuf[kind, t, core * 8 + eset, k] = part
+    def g_send(t, kind, *rows):
+        for k, row in enumerate(rows):
+            asend[kind, t, 0, pl.ds(k, 1)] = row
+            gbuf[kind, t, core * 8 + eset, pl.ds(k, 1)] = row
         for c, m in group:
-            tagged(asend.at[kind, t, 0, tiles], gbuf.at[kind, t, core * 8 + eset, tiles], AG + kind, t, flip_core(c), gpeer(m)).start()
-
-    def g_bytes(t, kind):
-        return gbuf.at[kind, t, pl.ds(0, 15), pl.ds(0, 2 if kind == ALPHA else 1)]
+            tagged(asend.at[kind, t, 0], gbuf.at[kind, t, core * 8 + eset], AG + kind, t, flip_core(c), gpeer(m)).start()
 
     def g_sum(t, kind):
-        came(g_bytes(t, kind), AG + kind, t)
-        return sum(gbuf[kind, t, j, 0] for j in range(16))
-
-    def r_send(t, kind, part):
-        asend[kind, t, 1, 0] = part
-        rbuf[kind, t, aset] = part
+        came(gbuf.at[kind, t, pl.ds(0, 15)], AG + kind, t)
+        both = [gbuf[kind, t, j] for j in range(16)]
+        return sum(both)[0:1], functools.reduce(jnp.maximum, both)[1:2]
+
+    def r_send(t, kind, row):
+        asend[kind, t, 1, pl.ds(0, 1)] = row
+        rbuf[kind, t, aset, pl.ds(0, 1)] = row
         for m in SEVEN:
-            tagged(asend.at[kind, t, 1, 0], rbuf.at[kind, t, aset], AR + kind, t, core, rpeer(m)).start()
+            tagged(asend.at[kind, t, 1], rbuf.at[kind, t, aset], AR + kind, t, core, rpeer(m)).start()
 
     def r_sum(t, kind):
         came(rbuf.at[kind, t, pl.ds(0, 7)], AR + kind, t)
-        return sum(rbuf[kind, t, j] for j in range(8))
-
-    def mean(tile):
-        return jnp.sum(jnp.sum(tile, axis=0, keepdims=True), axis=1, keepdims=True) / elems
+        return sum(rbuf[kind, t, j] for j in range(8))[0:1]
+
+    def mean(row):
+        return jnp.sum(row, axis=1, keepdims=True) / elems
 
     def total(t, kind):
-        tile = r_sum(t, kind)
-        sent(g_bytes(t, kind), AG + kind, t)
+        row = r_sum(t, kind)
+        sent(gbuf.at[kind, t, pl.ds(0, 15)], AG + kind, t)
         sent(rbuf.at[kind, t, pl.ds(0, 7)], AR + kind, t)
-        return mean(tile)
+        return mean(row)
 
     def put(t, kind, val):
         scal[kind, t] = jnp.broadcast_to(val, (8, LN))
 
     def get(t, kind):
         return scal[kind, t][0:1, 0:1]
+
+    def wide(tile, rows):
+        return jnp.concatenate([jnp.concatenate([tile] * PH, axis=1)] * (rows // 8), axis=0)
 
     def record(kind, t, s, val):
         rows = lax.broadcasted_iota(jnp.int32, (2, STEPS), 0)
@@ -221,11 +255,11 @@
             acc = acc + val * val
         parts.append(fold(acc))
     sums_out[...] = jnp.zeros(sums_out.shape, F32)
+    asend[...] = jnp.zeros(asend.shape, F32)
     pl.semaphore_wait(barrier, len(group) + len(SEVEN))
     for t in range(2):
         g_send(t, NORM, parts[t])
-    for m in SEVEN:
-        p_copy(0, m).start()
+    p_send(0)
     l_ld.wait()
 
     def perm_body(l, carry):
@@ -247,14 +281,15 @@
         return carry
 
     lax.fori_loop(0, mpo, perm_body, 0)
-    for n in range(2):
-        for j in range(3):
-            for d in NEAR:
-                l_copy(n, 0, j, d).start()
+    p_near(0)
+    l_sends = [(n, j) for n in range(2) for j in range(3)]
+    l_send(l_sends[:1])
+    p_last(0)
+    l_send(l_sends[1:])
     w0, w1, w2 = split3(wmat_ref[...])
     wpk[...] = jnp.concatenate([w0, w0, w0, w1, w1, w2], axis=1)
     for t in range(2):
-        r_send(t, NORM, g_sum(t, NORM))
+        r_send(t, NORM, g_sum(t, NORM)[0])
 
     def l_take(n, m, j, links):
         reg = l_region(n, m, j)
@@ -287,6 +322,8 @@
             l_take(n, a, j, (b, c))
             l_take(n, b, j, (c,))
             l_take(n, c, j, ())
+        if n:
+            p_send(1)
 
     def l_first():
         for n in range(2):
@@ -296,9 +333,9 @@
             for j in range(3):
                 a, b, c = ORDERS[j]
                 l_take(n, a + b, j, (c,))
-        for m in SEVEN:
-            p_copy(1, m).start()
+        p_near(1)
         l_rest(0)
+        p_last(1)
 
     def l_second():
         l_rest(1)
@@ -306,10 +343,6 @@
             sent(seven_l, LS, n)
             sent(near_l, LF, n)
             sent(far_l, LF + 1, n)
-
-    def psi_pass(t):
-        came(seven_psi, PS, t)
-        pf_copy(t).start()
 
     def ev_init(t):
         rinv = 1.0 / jnp.sqrt(total(t, NORM))
@@ -340,31 +373,34 @@
         if h:
             rows = pl.ds(pl.multiple_of(own, EC), EC)
             hv = gat[t, rows]
-            g_send(t, ALPHA, fold(hv * vec[t, s % 2, rows]) * get(t, FAC + s % 2), fold_max(jnp.abs(hv)))
+            g_send(t, ALPHA, fold(hv * vec[t, s % 2, rows]) * get(t, FAC + s % 2), fold(jnp.abs(hv), jnp.maximum))
 
         @pl.when(more)
         def _():
-            for m in SEVEN:
-                g_copy(t, h, m).start()
+            for k, m in ((0, NEAR), (1, FAR[::-1]), (1, NEAR)) if h else ((0, FAR[::-1]),):
+                for q in m:
+                    g_copy(t, k, q).start()
             fw_copy(t, h, 0).start()
 
         sent(rsb.at[t, h], RS + h, t)
 
-    def new_w(t, s, rows):
+    def new_w(t, s, first, count):
         cur, prev = s % 2, (s + 1) % 2
-        return gat[t, rows] - get(t, ALPHA) * get(t, FAC + cur) * vec[t, cur, rows] - get(t, BETA) * get(t, FAC + prev) * vec[t, prev, rows]
+        rows = pl.ds(pl.multiple_of(first, EC), count)
+        along, back = wide(scal[ALPHA, t] * scal[FAC + cur, t], count), wide(scal[BETA, t] * scal[FAC + prev, t], count)
+        return gat[t, rows] - along * vec[t, cur, rows] - back * vec[t, prev, rows]
 
     def ev_mid(t):
-        r_send(t, ALPHA, g_sum(t, ALPHA))
-        tile = functools.reduce(jnp.maximum, [gbuf[ALPHA, t, j, 1] for j in range(16)])
-        put(t, SIZE, jnp.max(jnp.max(tile, axis=0, keepdims=True), axis=1, keepdims=True))
+        row, most = g_sum(t, ALPHA)
+        r_send(t, ALPHA, row)
+        put(t, SIZE, jnp.max(most, axis=1, keepdims=True))
 
     def ev_alpha(t, s):
         alpha = total(t, ALPHA)
         put(t, ALPHA, alpha)
         put(t, SIZE, jnp.maximum(get(t, SIZE), jnp.maximum(jnp.abs(alpha), get(t, BETA))))
         record(0, t, s, alpha)
-        res = new_w(t, s, pl.ds(pl.multiple_of(own, EC), EC))
+        res = new_w(t, s, own, EC)
         g_send(t, BETA, fold(res * res))
 
         @pl.when(s == STEPS - 1)
@@ -377,7 +413,7 @@
             frecv[t, eset] = fsend[t, :, myrows]
 
     def ev_pass(t):
-        r_send(t, BETA, g_sum(t, BETA))
+        r_send(t, BETA, g_sum(t, BETA)[0])
 
     def ev_fwd(t, h):
         came(seven_halves, GA + h, t)
@@ -398,13 +434,13 @@
             outb[t, m, half_rows(0)] = outb[t, m, half_rows(0)] * fac
 
     def ev_vec(t, s):
-        size = get(t, SIZE)
-        rinv = jnp.where(size > 0, 1.0 / size, 0.0)
+        size = scal[SIZE, t]
+        rinv = wide(jnp.where(size > 0, 1.0 / size, 0.0), LN)
 
         def rows_of(first):
             def body(j, carry):
-                rows = pl.ds(pl.multiple_of(first + j * LN, LN), LN)
-                vec[t, (s + 1) % 2, rows] = new_w(t, s, rows) * rinv
+                start = first + j * LN
+                vec[t, (s + 1) % 2, pl.ds(pl.multiple_of(start, LN), LN)] = new_w(t, s, start, LN) * rinv
                 return carry
 
             lax.fori_loop(0, half // LN, body, 0)
@@ -418,12 +454,10 @@
             sent(seven_halves, GA + h, t)
 
     def r_phase(t, s, first, count):
-        rows = rf[:, pl.ds(pl.multiple_of(first, 16), count), :].reshape(mpo * count, bond)
-        xv = jnp.dot(rows, vec[t, s % 2], preferred_element_type=F32, precision=HI)
-        base = first % EH
+        xv = jnp.dot(rf[:, pl.ds(first, count), :].reshape(mpo * count, bond), vec[t, s % 2], preferred_element_type=F32, precision=HI)
         for r in range(mpo):
             for ij in range(PH):
-                xf[pl.ds(pl.multiple_of((ij * mpo + r) * NX + base, 8), count), :] = xv[r * count:(r + 1) * count, ij * LN:(ij + 1) * LN]
+                xf[pl.ds((ij * mpo + r) * NX + first % EH, count), :] = xv[r * count:(r + 1) * count, ij * LN:(ij + 1) * LN]
 
     def w_phase(h):
         for e in range(0, EH, 2):
@@ -433,95 +467,98 @@
             for q in range(2):
                 yf[pl.ds(h * EH + e + q, PH * mpo, stride=NY), :] = yv[:, q * LN:(q + 1) * LN]
 
-    def l_phase(t, s, h, n):
-        lhs = [jnp.concatenate([yf[pl.ds(pl.multiple_of((l * PH + mn) * NY + h * EH, 8), EH), :] for mn in range(PH)], axis=0) for l in range(mpo)]
+    def l_phase(t, h, n, fac):
+        lhs = [jnp.concatenate([yf[pl.ds((l * PH + mn) * NY + h * EH, EH), :] for mn in range(PH)], axis=0) for l in range(mpo)]
         y0, y1, y2 = split3(jnp.concatenate(lhs, axis=1))
         b0, b1, b2 = [l3[k, n].reshape(mpo * LN, PH * LN) for k in range(3)]
         p0 = jnp.dot(jnp.concatenate([y0, y1, y2], axis=0), b0, preferred_element_type=F32)
         p1 = jnp.dot(jnp.concatenate([y0, y1], axis=0), b1, preferred_element_type=F32)
         p2 = jnp.dot(y0, b2, preferred_element_type=F32)
-        ov = (((p0[2 * LN:] + p1[LN:]) + p2) + (p0[LN:2 * LN] + p1[:LN]) + p0[:LN]) * jnp.where(h == 1, get(t, FAC + s % 2), 1.0)
-        for j in range(PH):
-            m = FAR[j] + n * (CLOSE[j] - FAR[j])
+        ov = ((p0[2 * LN:] + p1[LN:]) + p2) + (p0[LN:2 * LN] + p1[:LN]) + p0[:LN]
+        if fac is not None:
+            ov = ov * fac
+        for j, m in enumerate(CLOSE if n else FAR):
             for mn in range(PH):
                 outb[t, m, half_rows(h), mn * LN:(mn + 1) * LN] = ov[mn * EH:(mn + 1) * EH, j * LN:(j + 1) * LN]
+
+    def send_part(t, h, part):
+        for m in part:
+            rs_copy(t, h, m).start()
+
+    quarter = EH // 2
 
     def step_body(it, carry):
         t, s = it % 2, it // 2
         ot = 1 - t
         os = (it + 1) // 2 - 1
-        first = 1 - (it + 2 * STEPS - 1) // (2 * STEPS)
-        has = it >= 1
-        more = jnp.logical_and(has, it < 2 * STEPS - 1)
-
-        @pl.when(it < 2)
+        more = it < 2 * STEPS - 1
+        later = it >= 2
+
+        @pl.when(it == 1)
         def _():
             ev_init(t)
 
-        @pl.when(it >= 2)
+        @pl.when(later)
         def _():
             ev_vec(t, s - 1)
 
-        @pl.when(it == 0)
+        r_phase(t, s, 0, quarter)
+
+        @pl.when(later)
         def _():
-            r_ld.wait()
-
-        def send_part(h, part):
-            for m in part:
-                rs_copy(t, h, m).start()
-
-        def slot_body(q, c2):
-            h = first * (q % 2) + (1 - first) * (q // 3)
-            n = first * ((q - 2) // 2) + (1 - first) * (q % 3 - 1)
-            is_rw = jnp.logical_or(jnp.logical_and(it == 0, q < 2), jnp.logical_and(has, q % 3 == 0))
-
-            def at(cond, slot, event, *args):
-                @pl.when(jnp.logical_and(cond, q == slot))
-                def _():
-                    event(*args)
-
-            @pl.when(is_rw)
-            def _():
-                def part(k, c3):
-                    r_phase(t, s, h * EH + k * (EH // 2), EH // 2)
-
-                    @pl.when(k == 0)
-                    def _():
-                        at(it == 0, 1, l_near, 1)
-                        at(it >= 2, 0, ev_pass, t)
-                        at(has, 0, ev_sum, ot, os, 0, more)
-                        at(has, 3, ev_mid, ot)
-                        at(it >= 2, 3, ev_scale, t, s)
-                        at(has, 3, send_part, 0, SEVEN)
-
-                    return c3
-
-                lax.fori_loop(0, 2, part, 0)
-                w_phase(h)
-                at(it == 0, 0, l_near, 0)
-                at(more, 3, ev_fwd, ot, 0)
-
-            @pl.when(jnp.logical_not(is_rw))
-            def _():
-                at(it == 0, 2, l_first)
-                at(it == 0, 4, l_second)
-                l_phase(t, s, h, n)
-                at(it == 0, 4, psi_pass, 1)
-                at(it == 0, 4, send_part, 0, SEVEN)
-                at(has, 1, ev_sum, ot, os, 1, more)
-                at(has, 4, ev_alpha, ot, os)
-                at(more, 4, ev_fwd, ot, 1)
-                at(has, 4, send_part, 1, FAR[::-1])
-                at(it == 0, 5, send_part, 1, FAR[::-1])
-                at(it >= 0, 5, send_part, 1, NEAR)
-
-            return c2
-
-        lax.fori_loop(0, 6, slot_body, 0)
+            ev_pass(t)
+
+        ev_sum(ot, os, 0, more)
+        r_phase(t, s, quarter, quarter)
+        w_phase(0)
+        l_phase(t, 0, 0, None)
+        ev_sum(ot, os, 1, more)
+        l_phase(t, 0, 1, None)
+        r_phase(t, s, EH, quarter)
+        ev_mid(ot)
+
+        @pl.when(later)
+        def _():
+            ev_scale(t, s)
+
+        send_part(t, 0, SEVEN)
+
+        r_phase(t, s, EH + quarter, quarter)
+        w_phase(1)
+        l_phase(t, 1, 0, get(t, FAC + s % 2))
+        ev_alpha(ot, os)
+
+        @pl.when(more)
+        def _():
+            ev_fwd(ot, 0)
+            ev_fwd(ot, 1)
+
+        send_part(t, 1, FAR[::-1])
+        l_phase(t, 1, 1, get(t, FAC + s % 2))
+        send_part(t, 1, NEAR)
         return carry
 
-    psi_pass(0)
-    lax.fori_loop(0, 2 * STEPS, step_body, 0)
+    p_rest(0)
+    ev_init(0)
+    r_ld.wait()
+    for h in range(2):
+        r_phase(0, 0, h * EH, quarter)
+        if h:
+            l_near(1)
+        r_phase(0, 0, h * EH + quarter, quarter)
+        w_phase(h)
+        if h == 0:
+            l_near(0)
+    l_first()
+    for n, part in enumerate((FAR[::-1], NEAR)):
+        for h in range(2):
+            l_phase(0, h, n, None)
+            send_part(0, h, part)
+            if n and not h:
+                p_rest(1)
+        if n == 0:
+            l_second()
+    lax.fori_loop(1, 2 * STEPS, step_body, 0)
 
     last = STEPS - 1
 
@@ -536,8 +573,8 @@
     ev_pass(0)
     ev_sum(1, last, 0, False)
     ev_sum(1, last, 1, False)
+    ev_mid(1)
     finish(0)
-    ev_mid(1)
     ev_alpha(1, last)
     ev_pass(1)
     finish(1)
@@ -568,7 +605,7 @@
             (2, 8, EC, WID),
             (2, 2, 7, EH, WID),
         ]
-        small = [(3, 2, 16, 2, 8, LN), (3, 2, 8, 8, LN), (3, 2, 2, 2, 8, LN), (SIZE + 1, 2, 8, LN), (2, 2, LN, LN), (2, 8, 2, 16, LN)]
+        small = [(3, 2, 16, 2, LN), (3, 2, 8, 2, LN), (3, 2, 2, 2, LN), (SIZE + 1, 2, 8, LN), (2, 2, LN, LN), (2, 8, 2, 16, LN)]
         call = pl.pallas_call(
             functools.partial(kernel, (bond, mpo, float(bond * bond * PH))),
             out_shape=[jax.ShapeDtypeStruct(shape, F32) for shape in (psi_loc.shape, (2, 2, STEPS))],
@@ -578,7 +615,7 @@
             + [pltpu.VMEM((3, 2, mpo, LN, WID), BF16), pltpu.VMEM((PH * mpo, 6 * PH * mpo), BF16)]
             + [pltpu.VMEM(shape, F32) for shape in small]
             + [dma((KINDS, 2))] * 2
-            + [dma((2, 3, 8)), dma((3,))],
+            + [dma((2, 3, 8)), dma((2, 3, 8)), dma((3,))],
             compiler_params=pltpu.CompilerParams(vmem_limit_bytes=63 << 20, has_side_effects=True, collective_id=0),
             name="lanczos",
         )

time: 273 us -> 252 us (0.923)
  Pallas kernels: 268 us -> 246 us
    pallas_call x1, Pallas kernels: 268 us -> 246 us  [local_run(): psi_next, sums = call(psi_loc, left_t, right_t, wmat)]
where the time goes in v5:
time: 252 us; the launch traced here: 251 us
  Pallas kernels  246 us (98%)
  local copies, waits for them, and re-layouts  4.63 us (2%)
    pallas_call x1, Pallas kernels, local_run(): psi_next, sums = call(psi_loc, left_t, right_t, wmat)  246 us

profile of v5, /device:TPU:1, one launch (start us, length us, event | category | flops | bytes accessed | tf_op | source)
XLA Modules:
  0.0 251.4 jit_solution(4600991069272294418)
XLA Ops:
  0.6 1.0 copy.9
  1.6 0.7 reshape.13.wmat_ref
  2.3 246.1 %lanczos.1 = (f32[2,16,2,2,512]{4,3,2,1,0:T(2,128)}, f32[2,2,4]{2,1,0:T(2,128)}) custom-call(f32[2,16,2,2,512]{4,3,2,1,0:T(2,128)} %psi_ref.1, f32[20,16,1024]{2,1,0:T(8,128)} %bitcast.11, f32[20,512,1024]{2,1,0:T(8,128)} %bitcast.10, f32[80,80]{1,0:T(8,128)} %reshape.13.wmat_ref), custom_call_target="tpu_custom_call" | custom-call | tf_op jit(solution)/shard_map/lanczos/pallas_call | solution.py:622
  248.4 1.3 slice_bitcast_fusion
  249.7 1.7 copy.11

commit v6 on v5

--- a/solution.py
+++ b/solution.py
@@ -13,6 +13,7 @@
 BF16 = jnp.bfloat16
 MESH = pl.DeviceIdType.MESH
 LN = 128
+RB = 16
 EC = 64
 EH = EC // 2
 PH = 4
@@ -29,7 +30,8 @@
 PS, PF, FI, AG = range(6, 10)
 AR = AG + 3
 LS, LF = AR + 3, AR + 4
-KINDS = AR + 6
+LR, PR = AR + 6, AR + 15
+KINDS = PR + 9
 THIRDS = ((0, 4), (4, 3), (7, 3))
 PLANES = ((0, 2), (2, 1), (3, 1))
 ORDERS = ((4, 2, 1), (2, 1, 4), (1, 4, 2))
@@ -49,6 +51,20 @@
     return (jnp.max if op is jnp.maximum else jnp.sum)(acc, axis=0, keepdims=True)
 
 
+def tree(j):
+    a, b, c = ORDERS[j]
+    return ((0, a), (0, b), (0, c)), ((a, b), (a, c), (b, c)), ((a + b, c),), ()
+
+
+def members(j):
+    a, b, c = ORDERS[j]
+    return NEAR, (a + b,), (a + c, b + c, a + b + c)
+
+
+def slot(m, j):
+    return 3 * [m in part for part in members(j)].index(True) + j
+
+
 def bits(m):
     return m // 4, (m // 2) % 2, m % 2
 
@@ -62,12 +78,12 @@
 
 
 def places(lb):
-    place = (lb // 16, (lb // 4) % 4, lb % 4)
-    return place, [q % 2 for q in place], [q // 2 for q in place], [((q + 1) // 2) % 2 for q in place]
-
-
-def kernel(cfg, psi_ref, left_ref, right_ref, wmat_ref, psi_out, sums_out,
-           rf, ls, lst, gat, vec, pg, praw, xf, yf, outb, rsb, l3, wpk, gbuf, rbuf, asend, scal, fsend, frecv, ssem, rsem, lsem, psem, ldsem):
+    place = (lb // RB, (lb // 4) % 4, lb % 4)
+    return place, [q % 2 for q in place], [q // 2 for q in place], [(q + 1) // 2 % 2 for q in place]
+
+
+def kernel(cfg, psi_ref, left_ref, right_ref, mpo_ref, rows_out, sums_out,
+           rf, ls, lst, gat, vec, pg, praw, wraw, wst, xf, yf, outb, rsb, l3, wpk, gbuf, rbuf, asend, scal, fsend, ssem, rsem, ldsem):
     bond, mpo, elems = cfg
     core, lb = lax.axis_index("rb"), lax.axis_index("lb")
     place, low, high, side = places(lb)
@@ -75,7 +91,7 @@
     half, lhalf = bond // 2, mpo // 2
     own = core * half + eset * EC
     other = 1 - core
-    myrows = pl.ds(pl.multiple_of(pos * 16, 16), 16)
+    myrows = pl.ds(pl.multiple_of(pos * RB, RB), RB)
     mycols = pl.ds(pl.multiple_of(core * half, half), half)
 
     def gpeer(m):
@@ -96,8 +112,8 @@
     def came(region, kind, t):
         tagged(region, region, kind, t, other, lb).wait_recv()
 
-    def half_rows(h):
-        return pl.ds(h * EH, EH)
+    def half_rows(h, base=0):
+        return pl.ds(base + h * EH if isinstance(h, int) else pl.multiple_of(base + h * EH, 8), EH)
 
     def rs_copy(t, h, m):
         return tagged(outb.at[t, m, half_rows(h)], rsb.at[t, h, m - 1], RS + h, t, core, rpeer(m))
@@ -117,72 +133,62 @@
     eight_halves = gat.at[0, pl.ds(0, 8 * EH)]
 
     def p_region(t, m, j):
-        return pg.at[t, pl.ds(*PLANES[j]), pl.ds(pl.multiple_of(flip(low, m) * 16, 16), 16), mycols]
+        return pg.at[t, pl.ds(*PLANES[j]), pl.ds(pl.multiple_of(flip(low, m) * RB, RB), RB), mycols]
 
     def p_copy(t, m, j, d):
         reg = p_region(t, m, j)
-        return remote(reg, reg, ssem.at[PS, t], psem.at[t, j, m + d], core, gpeer(d))
-
-    def p_take(t, m, j, links):
+        return remote(reg, reg, ssem.at[PS, t], rsem.at[PR + slot(m + d, j), t], core, gpeer(d))
+
+    def p_over(t, m, j):
         reg = p_region(t, m, j)
-        remote(reg, reg, ssem.at[PS, t], psem.at[t, j, m], core, lb).wait_recv()
-        for d in links:
+        return tagged(reg, reg, PF, t, other, lb)
+
+    def p_pass(t, level, j):
+        for m, d in tree(j)[level]:
             p_copy(t, m, j, d).start()
 
     def p_send(t):
         for j in range(3):
-            for d in NEAR:
-                p_copy(t, 0, j, d).start()
-
-    def p_near(t):
+            p_pass(t, 0, j)
+            p_over(t, 0, j).start()
+
+    def p_take(t, level):
         for j in range(3):
-            a, b, c = ORDERS[j]
-            p_take(t, a, j, (b, c))
-            p_take(t, b, j, (c,))
-
-    def p_last(t):
-        for j in range(3):
-            a, b, c = ORDERS[j]
-            p_take(t, a + b, j, (c,))
-
-    def p_rest(t):
-        for j in range(3):
-            a, b, c = ORDERS[j]
-            for m in (c, a + c, b + c, a + b + c):
-                p_take(t, m, j, ())
-        pf_copy(t).start()
-
-    def pf_copy(t):
-        reg = pg.at[t, :, :, mycols]
-        return tagged(reg, reg, PF, t, other, lb)
-
-    seven_psi = pg.at[0, :, pl.ds(0, 7 * 16), pl.ds(0, half)]
+            part = members(j)[level]
+            came(pg.at[t, pl.ds(0, PLANES[j][1]), pl.ds(0, RB * len(part)), pl.ds(0, half)], PR + 3 * level + j, t)
+            p_pass(t, level + 1, j)
+            for m in part:
+                p_over(t, m, j).start()
+
+    seven_psi = pg.at[0, :, pl.ds(0, 7 * RB), pl.ds(0, half)]
+    half_psi = pg.at[0, :, :, pl.ds(0, half)]
 
     def f_copy(t, m):
-        src = fsend.at[t, :, pl.ds(pl.multiple_of(flip(low, m) * 16, 16), 16)]
-        return tagged(src, frecv.at[t, eset], FI, t, core, gpeer(m))
-
-    seven_fin = frecv.at[0, pl.ds(0, 7)]
+        src = fsend.at[t, :, pl.ds(pl.multiple_of(flip(low, m) * RB, RB), RB)]
+        if m == 0:
+            return pltpu.make_async_copy(src, rows_out.at[t, eset], ldsem.at[t])
+        return tagged(src, rows_out.at[t, eset], FI, t, core, gpeer(m))
+
+    seven_fin = rows_out.at[0, pl.ds(0, 7)]
 
     def l_region(n, m, j):
         first, count = THIRDS[j]
-        return ls.at[n, pl.ds(core * lhalf + first, count), pl.ds(pl.multiple_of(flip(low, m) * 16, 16), 16)]
+        return ls.at[n, pl.ds(core * lhalf + first, count), pl.ds(pl.multiple_of(flip(low, m) * RB, RB), RB)]
 
     def l_copy(n, m, j, d):
         reg = l_region(n, m, j)
-        return remote(reg, reg, ssem.at[LS, n], lsem.at[n, j, m + d], core, gpeer(d))
-
-    def l_send(shares):
-        for n, j in shares:
-            for d in NEAR:
-                l_copy(n, 0, j, d).start()
+        return remote(reg, reg, ssem.at[LS, n], rsem.at[LR + slot(m + d, j), n], core, gpeer(d))
+
+    def l_pass(n, level, j):
+        for m, d in tree(j)[level]:
+            l_copy(n, m, j, d).start()
 
     def lf_copy(n, m, j):
         reg = l_region(n, m, j)
         return tagged(reg, reg, LF + (m in FAR), n, other, lb)
 
-    seven_l = ls.at[0, pl.ds(0, lhalf), pl.ds(0, 7 * 16)]
-    near_l, far_l = [ls.at[0, pl.ds(0, lhalf), pl.ds(0, len(part) * 16)] for part in (NEAR, FAR)]
+    seven_l = ls.at[0, pl.ds(0, lhalf), pl.ds(0, 7 * RB)]
+    near_l, far_l = [ls.at[0, pl.ds(0, lhalf), pl.ds(0, len(part) * RB)] for part in (NEAR, FAR)]
 
     group = [(c, m) for c in range(2) for m in range(8) if c or m]
 
@@ -198,7 +204,7 @@
 
     def g_sum(t, kind):
         came(gbuf.at[kind, t, pl.ds(0, 15)], AG + kind, t)
-        both = [gbuf[kind, t, j] for j in range(16)]
+        both = [gbuf[kind, t, j] for j in range(RB)]
         return sum(both)[0:1], functools.reduce(jnp.maximum, both)[1:2]
 
     def r_send(t, kind, row):
@@ -240,6 +246,8 @@
     l_ld.start()
     r_ld = pltpu.make_async_copy(right_ref.at[:, pl.ds(pl.multiple_of(eset * EC, EC), EC)], rf, ldsem.at[2])
     r_ld.start()
+    w_ld = pltpu.make_async_copy(mpo_ref, wraw, ldsem.at[3])
+    w_ld.start()
     barrier = pltpu.get_barrier_semaphore()
     for c, m in group:
         pl.semaphore_signal(barrier, inc=1, device_id=(flip_core(c), gpeer(m)), device_id_type=MESH)
@@ -263,7 +271,7 @@
     l_ld.wait()
 
     def perm_body(l, carry):
-        lane = lax.broadcasted_iota(jnp.int32, (16, LN), 1) // 32
+        lane = lax.broadcasted_iota(jnp.int32, (RB, LN), 1) // 32
         for hz in range(2):
             for hy in range(2):
                 src = [lst[l, :, pl.ds((4 * hz + 2 * q + hy) * LN, LN)] for q in range(2)]
@@ -281,27 +289,33 @@
         return carry
 
     lax.fori_loop(0, mpo, perm_body, 0)
-    p_near(0)
-    l_sends = [(n, j) for n in range(2) for j in range(3)]
-    l_send(l_sends[:1])
-    p_last(0)
-    l_send(l_sends[1:])
-    w0, w1, w2 = split3(wmat_ref[...])
-    wpk[...] = jnp.concatenate([w0, w0, w0, w1, w1, w2], axis=1)
+    p_take(0, 0)
+    shares = [(n, 0, j) for n in range(2) for j in range(3)]
+    l_pass(*shares[0])
     for t in range(2):
         r_send(t, NORM, g_sum(t, NORM)[0])
-
-    def l_take(n, m, j, links):
-        reg = l_region(n, m, j)
-        remote(reg, reg, ssem.at[LS, n], lsem.at[n, j, m], other, lb).wait_recv()
-        for d in links:
-            l_copy(n, m, j, d).start()
-        lf_copy(n, m, j).start()
+    p_take(0, 1)
+    for share in shares[1:]:
+        l_pass(*share)
+    w_ld.wait()
+    for mn in range(PH):
+        planes = [wraw[:, ij // 2, ij % 2, mn // 2, mn % 2, :] for ij in range(PH)]
+        wst[pl.ds(mn, mpo, stride=PH), :] = jnp.concatenate(planes + [jnp.zeros((mpo, LN - PH * mpo), F32)], axis=1)
+    w0, w1, w2 = split3(wst[:, :PH * mpo])
+    wpk[...] = jnp.concatenate([w0, w0, w0, w1, w1, w2], axis=1)
+
+    def l_take(n, level):
+        for j in range(3):
+            part = members(j)[level]
+            came(ls.at[n, pl.ds(0, THIRDS[j][1]), pl.ds(0, RB * len(part))], LR + 3 * level + j, n)
+            l_pass(n, level + 1, j)
+            for m in part:
+                lf_copy(n, m, j).start()
 
     def split_rows(n, offsets):
         def split_body(l, carry):
             for m in offsets:
-                rows = pl.ds(pl.multiple_of(flip(low, m) * 16, 16), 16)
+                rows = pl.ds(pl.multiple_of(flip(low, m) * RB, RB), RB)
                 for k, part in enumerate(split3(ls[n, l, rows])):
                     l3[k, n, l, rows] = part
             return carry
@@ -309,33 +323,18 @@
         lax.fori_loop(0, mpo, split_body, 0)
 
     def l_rest(n):
-        for j in range(3):
-            a, b, c = ORDERS[j]
-            for m in (a + c, b + c, a + b + c):
-                l_take(n, m, j, ())
         came(far_l, LF + 1, n)
         split_rows(n, FAR)
-
-    def l_near(n):
-        for j in range(3):
-            a, b, c = ORDERS[j]
-            l_take(n, a, j, (b, c))
-            l_take(n, b, j, (c,))
-            l_take(n, c, j, ())
-        if n:
-            p_send(1)
 
     def l_first():
         for n in range(2):
             came(near_l, LF, n)
             split_rows(n, CLOSE)
         for n in range(2):
-            for j in range(3):
-                a, b, c = ORDERS[j]
-                l_take(n, a + b, j, (c,))
-        p_near(1)
+            l_take(n, 1)
+        l_take(0, 2)
+        p_take(1, 0)
         l_rest(0)
-        p_last(1)
 
     def l_second():
         l_rest(1)
@@ -361,10 +360,10 @@
             lax.fori_loop(0, half // LN, tr_body, 0)
 
         turn(core * half)
-        pf_copy(t).wait_recv()
+        came(half_psi, PF, t)
         turn(other * half)
         sent(seven_psi, PS, t)
-        pf_copy(t).wait_send()
+        sent(half_psi, PF, t)
 
     def ev_sum(t, s, h, more):
         came(rsb.at[t, h], RS + h, t)
@@ -408,9 +407,8 @@
             for q in range(2):
                 pair = [res[:, j * LN:(j + 1) * LN] for j in (2 * q, 2 * q + 1)]
                 fsend[t, q] = jnp.concatenate(pair, axis=0).T
-            for m in SEVEN:
+            for m in SEVEN + (0,):
                 f_copy(t, m).start()
-            frecv[t, eset] = fsend[t, :, myrows]
 
     def ev_pass(t):
         r_send(t, BETA, g_sum(t, BETA)[0])
@@ -433,42 +431,40 @@
         for m in range(8):
             outb[t, m, half_rows(0)] = outb[t, m, half_rows(0)] * fac
 
-    def ev_vec(t, s):
+    def vec_rows(t, s, first):
         size = scal[SIZE, t]
         rinv = wide(jnp.where(size > 0, 1.0 / size, 0.0), LN)
-
-        def rows_of(first):
-            def body(j, carry):
-                start = first + j * LN
-                vec[t, (s + 1) % 2, pl.ds(pl.multiple_of(start, LN), LN)] = new_w(t, s, start, LN) * rinv
-                return carry
-
-            lax.fori_loop(0, half // LN, body, 0)
-
-        rows_of(core * half)
+        for j in range(0, half, LN):
+            vec[t, (s + 1) % 2, pl.ds(pl.multiple_of(first + j, LN), LN)] = new_w(t, s, first + j, LN) * rinv
+
+    def ev_vec(t, s):
         for h in range(2):
             came(eight_halves, FW + h, t)
-        rows_of(other * half)
+        vec_rows(t, s, other * half)
         for h in range(2):
             sent(eight_halves, FW + h, t)
             sent(seven_halves, GA + h, t)
 
-    def r_phase(t, s, first, count):
-        xv = jnp.dot(rf[:, pl.ds(first, count), :].reshape(mpo * count, bond), vec[t, s % 2], preferred_element_type=F32, precision=HI)
+    def rel(n, j):
+        return FAR[j] + n * (CLOSE[j] - FAR[j])
+
+    def r_phase(t, s, start, count, shift=0):
+        xv = jnp.dot(rf[:, pl.ds(start + shift, count), :].reshape(mpo * count, bond), vec[t, s % 2], preferred_element_type=F32, precision=HI)
         for r in range(mpo):
             for ij in range(PH):
-                xf[pl.ds((ij * mpo + r) * NX + first % EH, count), :] = xv[r * count:(r + 1) * count, ij * LN:(ij + 1) * LN]
-
-    def w_phase(h):
+                xf[pl.ds((ij * mpo + r) * NX + shift, count), :] = xv[r * count:(r + 1) * count, ij * LN:(ij + 1) * LN]
+
+    def w_phase(start):
         for e in range(0, EH, 2):
             xs = jnp.concatenate([xf[pl.ds(e + q, PH * mpo, stride=NX), :] for q in range(2)], axis=1)
             x0, x1, x2 = split3(xs)
             yv = jnp.dot(wpk[...], jnp.concatenate([x0, x1, x2, x0, x1, x0], axis=0), preferred_element_type=F32)
             for q in range(2):
-                yf[pl.ds(h * EH + e + q, PH * mpo, stride=NY), :] = yv[:, q * LN:(q + 1) * LN]
+                yf[pl.ds(start + e + q, PH * mpo, stride=NY), :] = yv[:, q * LN:(q + 1) * LN]
 
     def l_phase(t, h, n, fac):
-        lhs = [jnp.concatenate([yf[pl.ds((l * PH + mn) * NY + h * EH, EH), :] for mn in range(PH)], axis=0) for l in range(mpo)]
+        rows = [half_rows(h, (l * PH + mn) * NY) for l in range(mpo) for mn in range(PH)]
+        lhs = [jnp.concatenate([yf[r, :] for r in rows[l * PH:l * PH + PH]], axis=0) for l in range(mpo)]
         y0, y1, y2 = split3(jnp.concatenate(lhs, axis=1))
         b0, b1, b2 = [l3[k, n].reshape(mpo * LN, PH * LN) for k in range(3)]
         p0 = jnp.dot(jnp.concatenate([y0, y1, y2], axis=0), b0, preferred_element_type=F32)
@@ -477,9 +473,9 @@
         ov = ((p0[2 * LN:] + p1[LN:]) + p2) + (p0[LN:2 * LN] + p1[:LN]) + p0[:LN]
         if fac is not None:
             ov = ov * fac
-        for j, m in enumerate(CLOSE if n else FAR):
+        for j in range(PH):
             for mn in range(PH):
-                outb[t, m, half_rows(h), mn * LN:(mn + 1) * LN] = ov[mn * EH:(mn + 1) * EH, j * LN:(j + 1) * LN]
+                outb[t, rel(n, j), half_rows(h), mn * LN:(mn + 1) * LN] = ov[mn * EH:(mn + 1) * EH, j * LN:(j + 1) * LN]
 
     def send_part(t, h, part):
         for m in part:
@@ -509,7 +505,7 @@
             ev_pass(t)
 
         ev_sum(ot, os, 0, more)
-        r_phase(t, s, quarter, quarter)
+        r_phase(t, s, 0, quarter, quarter)
         w_phase(0)
         l_phase(t, 0, 0, None)
         ev_sum(ot, os, 1, more)
@@ -523,8 +519,8 @@
 
         send_part(t, 0, SEVEN)
 
-        r_phase(t, s, EH + quarter, quarter)
-        w_phase(1)
+        r_phase(t, s, EH, quarter, quarter)
+        w_phase(EH)
         l_phase(t, 1, 0, get(t, FAC + s % 2))
         ev_alpha(ot, os)
 
@@ -534,41 +530,75 @@
             ev_fwd(ot, 1)
 
         send_part(t, 1, FAR[::-1])
+        vec_rows(ot, os, core * half)
         l_phase(t, 1, 1, get(t, FAC + s % 2))
         send_part(t, 1, NEAR)
         return carry
 
-    p_rest(0)
+    p_take(0, 2)
     ev_init(0)
     r_ld.wait()
-    for h in range(2):
-        r_phase(0, 0, h * EH, quarter)
-        if h:
-            l_near(1)
-        r_phase(0, 0, h * EH + quarter, quarter)
-        w_phase(h)
-        if h == 0:
-            l_near(0)
+
+    def first_rw(h, carry):
+        start = pl.multiple_of(h * EH, EH)
+        r_phase(0, 0, start, quarter)
+
+        @pl.when(h == 1)
+        def _():
+            l_take(1, 0)
+            p_send(1)
+
+        r_phase(0, 0, start, quarter, quarter)
+        w_phase(start)
+
+        @pl.when(h == 0)
+        def _():
+            l_take(0, 0)
+
+        return carry
+
+    lax.fori_loop(0, 2, first_rw, 0)
     l_first()
-    for n, part in enumerate((FAR[::-1], NEAR)):
-        for h in range(2):
-            l_phase(0, h, n, None)
-            send_part(0, h, part)
-            if n and not h:
-                p_rest(1)
-        if n == 0:
+
+    def first_l(q, carry):
+        n, h = q // 2, q % 2
+
+        @pl.when(q == 2)
+        def _():
             l_second()
+
+        l_phase(0, h, n, None)
+        for j in range(3):
+            rs_copy(0, h, rel(n, j)).start()
+
+        @pl.when(n == 0)
+        def _():
+            rs_copy(0, h, FAR[3]).start()
+
+        @pl.when(q == 0)
+        def _():
+            p_take(1, 1)
+
+        @pl.when(q == 1)
+        def _():
+            l_take(1, 2)
+
+        @pl.when(q == 2)
+        def _():
+            p_take(1, 2)
+
+        return carry
+
+    lax.fori_loop(0, 4, first_l, 0)
     lax.fori_loop(1, 2 * STEPS, step_body, 0)
 
     last = STEPS - 1
 
     def finish(t):
-        rinv = 1.0 / ev_beta(t, last)
+        ev_beta(t, last)
         came(seven_fin, FI, t)
-        for i in range(2):
-            for j in range(2):
-                psi_out[t, :, i, j, :] = jnp.concatenate([frecv[t, g, i][:, j * EC:(j + 1) * EC] for g in range(8)], axis=1) * rinv
         sent(seven_fin, FI, t)
+        f_copy(t, 0).wait()
 
     ev_pass(0)
     ev_sum(1, last, 0, False)
@@ -580,6 +610,16 @@
     finish(1)
 
 
+def output_kernel(rows_ref, sums_ref, alpha_out, beta_out, psi_out):
+    alpha_out[...] = sums_ref[0]
+    beta_out[...] = sums_ref[1]
+    for t in range(2):
+        rinv = 1.0 / sums_ref[1, t:t + 1, STEPS - 1:STEPS]
+        for i in range(2):
+            for j in range(2):
+                psi_out[t, :, i, j, :] = jnp.concatenate([rows_ref[t, g, i][:, j * EC:(j + 1) * EC] for g in range(8)], axis=1) * rinv
+
+
 def solution(mesh):
     psi_spec = P(None, "lb", None, None, "rb")
 
@@ -588,7 +628,7 @@
         mpo, bond = left_loc.shape[1:]
         left_t = jnp.transpose(left_loc, (1, 0, 2))
         right_t = jnp.transpose(right_loc, (1, 0, 2))
-        wmat = jnp.transpose(mpo_pair.reshape(mpo, mpo, PH, PH), (0, 3, 2, 1)).reshape(PH * mpo, PH * mpo)
+        mpo_t = jnp.transpose(mpo_pair, (0, 2, 3, 4, 5, 1))
         dma = pltpu.SemaphoreType.DMA
         any_spec = pl.BlockSpec(memory_space=pl.ANY)
         vm = pl.BlockSpec(memory_space=pltpu.VMEM)
@@ -600,26 +640,36 @@
             (2, 2, bond, WID),
             (2, PH, LN, bond),
             psi_loc.shape,
+            mpo_t.shape,
+            (PH * mpo, LN),
             (PH * mpo * NX, LN),
             (PH * mpo * NY, LN),
             (2, 8, EC, WID),
             (2, 2, 7, EH, WID),
         ]
-        small = [(3, 2, 16, 2, LN), (3, 2, 8, 2, LN), (3, 2, 2, 2, LN), (SIZE + 1, 2, 8, LN), (2, 2, LN, LN), (2, 8, 2, 16, LN)]
+        small = [(3, 2, RB, 2, LN), (3, 2, 8, 2, LN), (3, 2, 2, 2, LN), (SIZE + 1, 2, 8, LN), (2, 2, LN, LN)]
         call = pl.pallas_call(
             functools.partial(kernel, (bond, mpo, float(bond * bond * PH))),
-            out_shape=[jax.ShapeDtypeStruct(shape, F32) for shape in (psi_loc.shape, (2, 2, STEPS))],
-            in_specs=[any_spec, any_spec, any_spec, vm],
-            out_specs=[vm] * 2,
+            out_shape=[jax.ShapeDtypeStruct(shape, F32) for shape in ((2, 8, 2, rows, LN), (2, 2, STEPS))],
+            in_specs=[any_spec] * 4,
+            out_specs=[any_spec, vm],
             scratch_shapes=[pltpu.VMEM(shape, F32) for shape in f32_shapes]
             + [pltpu.VMEM((3, 2, mpo, LN, WID), BF16), pltpu.VMEM((PH * mpo, 6 * PH * mpo), BF16)]
             + [pltpu.VMEM(shape, F32) for shape in small]
             + [dma((KINDS, 2))] * 2
-            + [dma((2, 3, 8)), dma((2, 3, 8)), dma((3,))],
+            + [dma((4,))],
             compiler_params=pltpu.CompilerParams(vmem_limit_bytes=63 << 20, has_side_effects=True, collective_id=0),
             name="lanczos",
         )
-        psi_next, sums = call(psi_loc, left_t, right_t, wmat)
-        return sums[0], sums[1], psi_next
+        last_rows, sums = call(psi_loc, left_t, right_t, mpo_t)
+        shapes = [(2, STEPS), (2, STEPS), psi_loc.shape]
+        put_out = pl.pallas_call(
+            output_kernel,
+            out_shape=[jax.ShapeDtypeStruct(shape, F32) for shape in shapes],
+            in_specs=[vm] * 2,
+            out_specs=[vm] * 3,
+            name="outputs",
+        )
+        return put_out(last_rows, sums)
 
     return jax.shard_map(local_run, mesh=mesh, in_specs=(psi_spec, P("lb", None, None), P("rb", None, None), P()), out_specs=(P(), P(), psi_spec), check_vma=False)

time: 252 us -> 245 us (0.972)
  local copies, waits for them, and re-layouts: 4.63 us -> 0 us
    pallas_call x1 -> x2, Pallas kernels: 246 us -> 244 us  [the longest x1 242 us: local_run(): last_rows, sums = call(psi_loc, left_t, right_t, mpo_t)]
where the time goes in v6:
time: 245 us; the launch traced here: 244 us
  Pallas kernels  244 us (100%)
    pallas_call x1, Pallas kernels, local_run(): last_rows, sums = call(psi_loc, left_t, right_t, mpo_t)  242 us

profile of v6, /device:TPU:1, one launch (start us, length us, event | category | flops | bytes accessed | tf_op | source)
XLA Modules:
  0.0 244.4 jit_solution(16372367673159911791)
XLA Ops:
  0.6 241.9 %lanczos.1 = (f32[2,8,2,16,128]{4,3,2,1,0:T(8,128)}, f32[2,2,4]{2,1,0:T(2,128)}) custom-call(f32[2,16,2,2,512]{4,3,2,1,0:T(2,128)} %psi_ref.1, f32[20,16,1024]{2,1,0:T(8,128)} %bitcast.4, f32[20,512,1024]{2,1,0:T(8,128)} %bitcast.3, f32[20,2,2,2,2,20]{5,4,3,2,1,0:T(2,128)} %bitcast.5), custom_call_target="tpu_custom_call" | custom-call | tf_op jit(solution)/shard_map/lanczos/pallas_call | solution.py:664
  242.6 1.8 outputs.1

commit v7 on v6

--- a/solution.py
+++ b/solution.py
@@ -12,6 +12,7 @@
 F32 = jnp.float32
 BF16 = jnp.bfloat16
 MESH = pl.DeviceIdType.MESH
+BOTH, SHARES, EIGHT = range(2), range(3), range(8)
 LN = 128
 RB = 16
 EC = 64
@@ -29,12 +30,15 @@
 RS, GA, FW = 0, 2, 4
 PS, PF, FI, AG = range(6, 10)
 AR = AG + 3
-LS, LF = AR + 3, AR + 4
-LR, PR = AR + 6, AR + 15
-KINDS = PR + 9
+LS, LF, EX = AR + 3, AR + 6, AR + 9
+PR, LR = EX + 2, EX + 11
+KINDS = LR + 12
+SIDE, MAIN, DIAG = SHARES
 THIRDS = ((0, 4), (4, 3), (7, 3))
 PLANES = ((0, 2), (2, 1), (3, 1))
-ORDERS = ((4, 2, 1), (2, 1, 4), (1, 4, 2))
+ORDERS = (NEAR, NEAR[1:] + NEAR[:1], NEAR[2:] + NEAR[:2])
+PIECES = (SIDE,) * 3 + (MAIN,) * 3 + (DIAG,) * 2
+SIDES, MAINS, DIAGS = [[u for u, ph in enumerate(PIECES) if ph == phase] for phase in SHARES]
 
 
 def split3(val):
@@ -61,12 +65,12 @@
     return NEAR, (a + b,), (a + c, b + c, a + b + c)
 
 
-def slot(m, j):
-    return 3 * [m in part for part in members(j)].index(True) + j
+def slot(m, j, step=3):
+    return step * [m in part for part in members(j)].index(True) + j
 
 
 def bits(m):
-    return m // 4, (m // 2) % 2, m % 2
+    return [m // d % 2 for d in NEAR]
 
 
 def number(trip, base=2):
@@ -83,7 +87,7 @@
 
 
 def kernel(cfg, psi_ref, left_ref, right_ref, mpo_ref, rows_out, sums_out,
-           rf, ls, lst, gat, vec, pg, praw, wraw, wst, xf, yf, outb, rsb, l3, wpk, gbuf, rbuf, asend, scal, fsend, ssem, rsem, ldsem):
+           rf, ls, lst, gat, vec, pg, praw, wraw, wst, xf, yf, outb, rsb, xst, l3, wpk, gbuf, rbuf, asend, scal, fsend, ssem, rsem, ldsem):
     bond, mpo, elems = cfg
     core, lb = lax.axis_index("rb"), lax.axis_index("lb")
     place, low, high, side = places(lb)
@@ -94,6 +98,9 @@
     myrows = pl.ds(pl.multiple_of(pos * RB, RB), RB)
     mycols = pl.ds(pl.multiple_of(core * half, half), half)
 
+    def chip_rows(m):
+        return pl.ds(pl.multiple_of(flip(low, m) * RB, RB), RB)
+
     def gpeer(m):
         return number([q + b * (1 - 2 * p) for q, b, p in zip(place, bits(m), low)], 4)
 
@@ -111,6 +118,9 @@
 
     def came(region, kind, t):
         tagged(region, region, kind, t, other, lb).wait_recv()
+
+    def came_at(region, arrival):
+        remote(region, region, ssem.at[0, 0], arrival, other, lb).wait_recv()
 
     def half_rows(h, base=0):
         return pl.ds(base + h * EH if isinstance(h, int) else pl.multiple_of(base + h * EH, 8), EH)
@@ -133,7 +143,7 @@
     eight_halves = gat.at[0, pl.ds(0, 8 * EH)]
 
     def p_region(t, m, j):
-        return pg.at[t, pl.ds(*PLANES[j]), pl.ds(pl.multiple_of(flip(low, m) * RB, RB), RB), mycols]
+        return pg.at[t, pl.ds(*PLANES[j]), chip_rows(m), mycols]
 
     def p_copy(t, m, j, d):
         reg = p_region(t, m, j)
@@ -148,12 +158,12 @@
             p_copy(t, m, j, d).start()
 
     def p_send(t):
-        for j in range(3):
+        for j in SHARES:
             p_pass(t, 0, j)
             p_over(t, 0, j).start()
 
     def p_take(t, level):
-        for j in range(3):
+        for j in SHARES:
             part = members(j)[level]
             came(pg.at[t, pl.ds(0, PLANES[j][1]), pl.ds(0, RB * len(part)), pl.ds(0, half)], PR + 3 * level + j, t)
             p_pass(t, level + 1, j)
@@ -164,33 +174,53 @@
     half_psi = pg.at[0, :, :, pl.ds(0, half)]
 
     def f_copy(t, m):
-        src = fsend.at[t, :, pl.ds(pl.multiple_of(flip(low, m) * RB, RB), RB)]
+        src = fsend.at[t, :, chip_rows(m)]
         if m == 0:
             return pltpu.make_async_copy(src, rows_out.at[t, eset], ldsem.at[t])
         return tagged(src, rows_out.at[t, eset], FI, t, core, gpeer(m))
 
     seven_fin = rows_out.at[0, pl.ds(0, 7)]
 
-    def l_region(n, m, j):
-        first, count = THIRDS[j]
-        return ls.at[n, pl.ds(core * lhalf + first, count), pl.ds(pl.multiple_of(flip(low, m) * RB, RB), RB)]
-
-    def l_copy(n, m, j, d):
-        reg = l_region(n, m, j)
-        return remote(reg, reg, ssem.at[LS, n], rsem.at[LR + slot(m + d, j), n], core, gpeer(d))
-
-    def l_pass(n, level, j):
-        for m, d in tree(j)[level]:
-            l_copy(n, m, j, d).start()
-
-    def lf_copy(n, m, j):
-        reg = l_region(n, m, j)
-        return tagged(reg, reg, LF + (m in FAR), n, other, lb)
-
-    seven_l = ls.at[0, pl.ds(0, lhalf), pl.ds(0, 7 * RB)]
-    near_l, far_l = [ls.at[0, pl.ds(0, lhalf), pl.ds(0, len(part) * RB)] for part in (NEAR, FAR)]
-
-    group = [(c, m) for c in range(2) for m in range(8) if c or m]
+    fifth = lhalf // 2
+    pieces = [(1, core * lhalf + fifth * high[k], fifth, k * LN, LN, k) for k in SHARES]
+    pieces += [(0, core * lhalf + first, count, 0, WID, k) for k, (first, count) in enumerate(THIRDS)]
+    pieces += [(1, core * lhalf + fifth * k, fifth, 3 * LN, LN, 2 - k) for k in BOTH]
+
+    def l_region(u, m):
+        n, first, count, lane, lanes, _ = pieces[u]
+        return ls.at[n, pl.ds(first, count), chip_rows(m), pl.ds(lane, lanes)]
+
+    def l_arrival(u, level):
+        return rsem.at[LR + (3 * u + level) // 2, (3 * u + level) % 2]
+
+    def l_copy(u, m, d):
+        reg = l_region(u, m)
+        return remote(reg, reg, ssem.at[LS + PIECES[u], 0], l_arrival(u, slot(m + d, pieces[u][5], 1) - pieces[u][5]), core, gpeer(d))
+
+    def l_pass(level, *which):
+        for u in which:
+            for m, d in tree(pieces[u][5])[level]:
+                l_copy(u, m, d).start()
+
+    def lf_copy(u, m):
+        reg = l_region(u, m)
+        return tagged(reg, reg, LF + PIECES[u], int(m in FAR), other, lb)
+
+    def l_bytes(phase, rows):
+        count, lanes = ((fifth, 3 * LN), (lhalf, WID), (lhalf, LN))[phase]
+        return ls.at[0, pl.ds(0, count), pl.ds(0, rows), pl.ds(0, lanes)]
+
+    def ex_region(k, mine):
+        bit = high[k] if mine else 1 - high[k]
+        return ls.at[1, pl.ds(core * lhalf + fifth * bit, fifth), :, pl.ds(k * LN, LN)]
+
+    def ex_copy(k):
+        return tagged(xst.at[k], ex_region(k, True), EX, 0, core, rpeer(NEAR[k]))
+
+    def ex_over(k):
+        return tagged(ex_region(k, False), ex_region(k, False), EX, 1, other, lb)
+
+    group = [(c, m) for c in BOTH for m in EIGHT if c or m]
 
     def flip_core(c):
         return core + c * (1 - 2 * core)
@@ -215,7 +245,7 @@
 
     def r_sum(t, kind):
         came(rbuf.at[kind, t, pl.ds(0, 7)], AR + kind, t)
-        return sum(rbuf[kind, t, j] for j in range(8))[0:1]
+        return sum(rbuf[kind, t, j] for j in EIGHT)[0:1]
 
     def mean(row):
         return jnp.sum(row, axis=1, keepdims=True) / elems
@@ -255,7 +285,7 @@
         pl.semaphore_signal(barrier, inc=1, device_id=(core, rpeer(m)), device_id_type=MESH)
     psi_ld.wait()
     parts = []
-    for t in range(2):
+    for t in BOTH:
         acc = 0
         for ij in range(PH):
             val = praw[t, :, ij // 2, ij % 2, :]
@@ -265,17 +295,17 @@
     sums_out[...] = jnp.zeros(sums_out.shape, F32)
     asend[...] = jnp.zeros(asend.shape, F32)
     pl.semaphore_wait(barrier, len(group) + len(SEVEN))
-    for t in range(2):
+    for t in BOTH:
         g_send(t, NORM, parts[t])
     p_send(0)
     l_ld.wait()
 
     def perm_body(l, carry):
         lane = lax.broadcasted_iota(jnp.int32, (RB, LN), 1) // 32
-        for hz in range(2):
-            for hy in range(2):
-                src = [lst[l, :, pl.ds((4 * hz + 2 * q + hy) * LN, LN)] for q in range(2)]
-                for hx in range(2):
+        for hz in BOTH:
+            for hy in BOTH:
+                src = [lst[l, :, pl.ds((4 * hz + 2 * q + hy) * LN, LN)] for q in BOTH]
+                for hx in BOTH:
                     pick = None
                     for c in range(PH):
                         shift = (c - 2 * (c % 2) - hx) * 32 % LN
@@ -285,68 +315,100 @@
                     far = sum(rel) // 2
                     rank = [p + far * (1 - 2 * p) for p in rel]
                     j = 3 - (3 * rank[0] + 2 * rank[1] + rank[2])
-                    ls[1 - far, l, myrows, pl.ds(pl.multiple_of(j * LN, LN), LN)] = pick
+                    one = sum(rel) % 2 - sum(rel) // 3
+                    here, there = l // fifth % 2, sum(p * q for p, q in zip(rel, high))
+                    skip = one * (here + there - 2 * here * there)
+                    ls[1 - far, l + skip * (mpo - l), myrows, pl.ds(pl.multiple_of(j * LN, LN), LN)] = pick
         return carry
 
     lax.fori_loop(0, mpo, perm_body, 0)
     p_take(0, 0)
-    shares = [(n, 0, j) for n in range(2) for j in range(3)]
-    l_pass(*shares[0])
-    for t in range(2):
+    l_pass(0, *SIDES)
+    for t in BOTH:
         r_send(t, NORM, g_sum(t, NORM)[0])
     p_take(0, 1)
-    for share in shares[1:]:
-        l_pass(*share)
+    l_pass(0, *MAINS[:1])
     w_ld.wait()
     for mn in range(PH):
         planes = [wraw[:, ij // 2, ij % 2, mn // 2, mn % 2, :] for ij in range(PH)]
         wst[pl.ds(mn, mpo, stride=PH), :] = jnp.concatenate(planes + [jnp.zeros((mpo, LN - PH * mpo), F32)], axis=1)
     w0, w1, w2 = split3(wst[:, :PH * mpo])
-    wpk[...] = jnp.concatenate([w0, w0, w0, w1, w1, w2], axis=1)
-
-    def l_take(n, level):
-        for j in range(3):
+    none = jnp.zeros_like(w0)
+    groups = [jnp.concatenate(g, axis=1) for g in ([w0] * 3, [w1, w1, none], [w2, none, none])]
+    wpk[...] = jnp.concatenate(groups, axis=0)
+
+    def l_take(level, *which):
+        for u in which:
+            n, _, count, _, lanes, j = pieces[u]
             part = members(j)[level]
-            came(ls.at[n, pl.ds(0, THIRDS[j][1]), pl.ds(0, RB * len(part))], LR + 3 * level + j, n)
-            l_pass(n, level + 1, j)
+            came_at(ls.at[n, pl.ds(0, count), pl.ds(0, RB * len(part)), pl.ds(0, lanes)], l_arrival(u, level))
+            l_pass(level + 1, u)
             for m in part:
-                lf_copy(n, m, j).start()
-
-    def split_rows(n, offsets):
+                lf_copy(u, m).start()
+
+    def split_rows(n, lane, lanes, offsets):
+        cols = pl.ds(lane, lanes)
+
         def split_body(l, carry):
             for m in offsets:
-                rows = pl.ds(pl.multiple_of(flip(low, m) * RB, RB), RB)
-                for k, part in enumerate(split3(ls[n, l, rows])):
-                    l3[k, n, l, rows] = part
+                rows = chip_rows(m)
+                for k, part in enumerate(split3(ls[n, l, rows, cols])):
+                    l3[k, n, l, rows, cols] = part
             return carry
 
         lax.fori_loop(0, mpo, split_body, 0)
 
-    def l_rest(n):
-        came(far_l, LF + 1, n)
-        split_rows(n, FAR)
+    def over(phase, part):
+        came(l_bytes(phase, RB * len(part)), LF + phase, int(part is FAR))
+
+    def ex_send():
+        def turn_body(i, carry):
+            for k in SHARES:
+                xst[k, i] = ls[1, core * lhalf + fifth * high[k] + i, :, k * LN:(k + 1) * LN].T
+            return carry
+
+        lax.fori_loop(0, fifth, turn_body, 0)
+        for k in SHARES:
+            ex_copy(k).start()
+
+    def ex_take():
+        came(l_bytes(SIDE, LN), EX, 0)
+        for k in SHARES:
+            ex_over(k).start()
 
     def l_first():
-        for n in range(2):
-            came(near_l, LF, n)
-            split_rows(n, CLOSE)
-        for n in range(2):
-            l_take(n, 1)
-        l_take(0, 2)
+        l_take(2, *SIDES)
+        ex_send()
+        over(MAIN, NEAR)
+        split_rows(0, 0, WID, CLOSE)
+        l_take(1, *(MAINS + DIAGS))
+        p_send(1)
+        ex_take()
+        l_take(2, *MAINS)
+        for part in (NEAR, FAR):
+            over(SIDE, part)
+        came(l_bytes(SIDE, LN), EX, 1)
+        split_rows(1, 0, 3 * LN, CLOSE + FAR)
+        over(MAIN, FAR)
+        split_rows(0, 0, WID, FAR)
         p_take(1, 0)
-        l_rest(0)
+        l_take(2, *DIAGS)
 
     def l_second():
-        l_rest(1)
-        for n in range(2):
-            sent(seven_l, LS, n)
-            sent(near_l, LF, n)
-            sent(far_l, LF + 1, n)
+        for part in (NEAR, FAR):
+            over(DIAG, part)
+        split_rows(1, 3 * LN, LN, CLOSE + FAR)
+        for phase in SHARES:
+            sent(l_bytes(phase, 7 * RB), LS + phase, 0)
+            for k, part in enumerate((NEAR, FAR)):
+                sent(l_bytes(phase, RB * len(part)), LF + phase, k)
+        for k in BOTH:
+            sent(l_bytes(SIDE, LN), EX, k)
 
     def ev_init(t):
         rinv = 1.0 / jnp.sqrt(total(t, NORM))
         put(t, BETA, jnp.zeros((1, 1), F32))
-        for slot in range(2):
+        for slot in BOTH:
             put(t, FAC + slot, jnp.ones((1, 1), F32))
 
         def turn(first):
@@ -404,7 +466,7 @@
 
         @pl.when(s == STEPS - 1)
         def _():
-            for q in range(2):
+            for q in BOTH:
                 pair = [res[:, j * LN:(j + 1) * LN] for j in (2 * q, 2 * q + 1)]
                 fsend[t, q] = jnp.concatenate(pair, axis=0).T
             for m in SEVEN + (0,):
@@ -428,7 +490,7 @@
     def ev_scale(t, s):
         ev_beta(t, s - 1)
         fac = get(t, FAC + s % 2)
-        for m in range(8):
+        for m in EIGHT:
             outb[t, m, half_rows(0)] = outb[t, m, half_rows(0)] * fac
 
     def vec_rows(t, s, first):
@@ -438,10 +500,10 @@
             vec[t, (s + 1) % 2, pl.ds(pl.multiple_of(first + j, LN), LN)] = new_w(t, s, first + j, LN) * rinv
 
     def ev_vec(t, s):
-        for h in range(2):
+        for h in BOTH:
             came(eight_halves, FW + h, t)
         vec_rows(t, s, other * half)
-        for h in range(2):
+        for h in BOTH:
             sent(eight_halves, FW + h, t)
             sent(seven_halves, GA + h, t)
 
@@ -456,17 +518,18 @@
 
     def w_phase(start):
         for e in range(0, EH, 2):
-            xs = jnp.concatenate([xf[pl.ds(e + q, PH * mpo, stride=NX), :] for q in range(2)], axis=1)
+            xs = jnp.concatenate([xf[pl.ds(e + q, PH * mpo, stride=NX), :] for q in BOTH], axis=1)
             x0, x1, x2 = split3(xs)
-            yv = jnp.dot(wpk[...], jnp.concatenate([x0, x1, x2, x0, x1, x0], axis=0), preferred_element_type=F32)
-            for q in range(2):
+            y0, y1, y2 = jnp.split(jnp.dot(wpk[...], jnp.concatenate([x0, x1, x2], axis=0), preferred_element_type=F32), 3)
+            yv = (y2 + y1) + y0
+            for q in BOTH:
                 yf[pl.ds(start + e + q, PH * mpo, stride=NY), :] = yv[:, q * LN:(q + 1) * LN]
 
     def l_phase(t, h, n, fac):
         rows = [half_rows(h, (l * PH + mn) * NY) for l in range(mpo) for mn in range(PH)]
         lhs = [jnp.concatenate([yf[r, :] for r in rows[l * PH:l * PH + PH]], axis=0) for l in range(mpo)]
         y0, y1, y2 = split3(jnp.concatenate(lhs, axis=1))
-        b0, b1, b2 = [l3[k, n].reshape(mpo * LN, PH * LN) for k in range(3)]
+        b0, b1, b2 = [l3[k, n].reshape(mpo * LN, PH * LN) for k in SHARES]
         p0 = jnp.dot(jnp.concatenate([y0, y1, y2], axis=0), b0, preferred_element_type=F32)
         p1 = jnp.dot(jnp.concatenate([y0, y1], axis=0), b1, preferred_element_type=F32)
         p2 = jnp.dot(y0, b2, preferred_element_type=F32)
@@ -536,6 +599,8 @@
         return carry
 
     p_take(0, 2)
+    l_take(0, *SIDES)
+    l_pass(0, *(MAINS[1:] + DIAGS))
     ev_init(0)
     r_ld.wait()
 
@@ -545,15 +610,14 @@
 
         @pl.when(h == 1)
         def _():
-            l_take(1, 0)
-            p_send(1)
+            l_take(0, *(MAINS + DIAGS))
 
         r_phase(0, 0, start, quarter, quarter)
         w_phase(start)
 
         @pl.when(h == 0)
         def _():
-            l_take(0, 0)
+            l_take(1, *SIDES)
 
         return carry
 
@@ -568,20 +632,16 @@
             l_second()
 
         l_phase(0, h, n, None)
-        for j in range(3):
+        for j in SHARES:
             rs_copy(0, h, rel(n, j)).start()
 
         @pl.when(n == 0)
         def _():
             rs_copy(0, h, FAR[3]).start()
 
-        @pl.when(q == 0)
+        @pl.when(q == 1)
         def _():
             p_take(1, 1)
-
-        @pl.when(q == 1)
-        def _():
-            l_take(1, 2)
 
         @pl.when(q == 2)
         def _():
@@ -613,11 +673,11 @@
 def output_kernel(rows_ref, sums_ref, alpha_out, beta_out, psi_out):
     alpha_out[...] = sums_ref[0]
     beta_out[...] = sums_ref[1]
-    for t in range(2):
+    for t in BOTH:
         rinv = 1.0 / sums_ref[1, t:t + 1, STEPS - 1:STEPS]
-        for i in range(2):
-            for j in range(2):
-                psi_out[t, :, i, j, :] = jnp.concatenate([rows_ref[t, g, i][:, j * EC:(j + 1) * EC] for g in range(8)], axis=1) * rinv
+        for i in BOTH:
+            for j in BOTH:
+                psi_out[t, :, i, j, :] = jnp.concatenate([rows_ref[t, g, i][:, j * EC:(j + 1) * EC] for g in EIGHT], axis=1) * rinv
 
 
 def solution(mesh):
@@ -634,7 +694,7 @@
         vm = pl.BlockSpec(memory_space=pltpu.VMEM)
         f32_shapes = [
             (mpo, EC, bond),
-            (2, mpo, LN, WID),
+            (2, mpo + 1, LN, WID),
             (mpo, rows, bond),
             (2, bond, WID),
             (2, 2, bond, WID),
@@ -646,15 +706,16 @@
             (PH * mpo * NY, LN),
             (2, 8, EC, WID),
             (2, 2, 7, EH, WID),
+            (3, mpo // 4, LN, LN),
         ]
-        small = [(3, 2, RB, 2, LN), (3, 2, 8, 2, LN), (3, 2, 2, 2, LN), (SIZE + 1, 2, 8, LN), (2, 2, LN, LN)]
+        small = [(3, 2, k, 2, LN) for k in (RB, 8, 2)] + [(SIZE + 1, 2, 8, LN), (2, 2, LN, LN)]
         call = pl.pallas_call(
             functools.partial(kernel, (bond, mpo, float(bond * bond * PH))),
-            out_shape=[jax.ShapeDtypeStruct(shape, F32) for shape in ((2, 8, 2, rows, LN), (2, 2, STEPS))],
+            out_shape=[jax.ShapeDtypeStruct(shape, F32) for shape in ((2, len(EIGHT), 2, rows, LN), (2, 2, STEPS))],
             in_specs=[any_spec] * 4,
             out_specs=[any_spec, vm],
             scratch_shapes=[pltpu.VMEM(shape, F32) for shape in f32_shapes]
-            + [pltpu.VMEM((3, 2, mpo, LN, WID), BF16), pltpu.VMEM((PH * mpo, 6 * PH * mpo), BF16)]
+            + [pltpu.VMEM((3, 2, mpo, LN, WID), BF16), pltpu.VMEM((3 * PH * mpo, 3 * PH * mpo), BF16)]
             + [pltpu.VMEM(shape, F32) for shape in small]
             + [dma((KINDS, 2))] * 2
             + [dma((4,))],

time: 245 us -> 236 us (0.963)
  Pallas kernels: 244 us -> 236 us
    pallas_call x1, Pallas kernels: 242 us -> 234 us  [local_run(): last_rows, sums = call(psi_loc, left_t, right_t, mpo_t)]
where the time goes in v7:
time: 236 us
  Pallas kernels  236 us (100%)
    pallas_call x1, Pallas kernels, local_run(): last_rows, sums = call(psi_loc, left_t, right_t, mpo_t)  234 us

profile of v7, /device:TPU:1, one launch (start us, length us, event | category | flops | bytes accessed | tf_op | source)
XLA Modules:
  0.0 236.2 jit_solution(10053017528538800993)
XLA Ops:
  0.6 233.8 %lanczos.1 = (f32[2,8,2,16,128]{4,3,2,1,0:T(8,128)}, f32[2,2,4]{2,1,0:T(2,128)}) custom-call(f32[2,16,2,2,512]{4,3,2,1,0:T(2,128)} %psi_ref.1, f32[20,16,1024]{2,1,0:T(8,128)} %bitcast.4, f32[20,512,1024]{2,1,0:T(8,128)} %bitcast.3, f32[20,2,2,2,2,20]{5,4,3,2,1,0:T(2,128)} %bitcast.5), custom_call_target="tpu_custom_call" | custom-call | tf_op jit(solution)/shard_map/lanczos/pallas_call | solution.py:725
  234.4 1.8 outputs.1

commit v8 on v7

--- a/solution.py
+++ b/solution.py
@@ -35,7 +35,7 @@
 KINDS = LR + 12
 SIDE, MAIN, DIAG = SHARES
 THIRDS = ((0, 4), (4, 3), (7, 3))
-PLANES = ((0, 2), (2, 1), (3, 1))
+PLANES = ((0, 2), (2, 1), (3, 1)), ((0, 1), (1, 2), (3, 1))
 ORDERS = (NEAR, NEAR[1:] + NEAR[:1], NEAR[2:] + NEAR[:2])
 PIECES = (SIDE,) * 3 + (MAIN,) * 3 + (DIAG,) * 2
 SIDES, MAINS, DIAGS = [[u for u, ph in enumerate(PIECES) if ph == phase] for phase in SHARES]
@@ -135,15 +135,14 @@
         reg = gat.at[t, gat_rows(0, h)]
         return tagged(reg, reg, GA + h, t, core, gpeer(m))
 
-    def fw_copy(t, h, m):
-        reg = gat.at[t, gat_rows(m, h)]
-        return tagged(reg, reg, FW + h, t, other, lb)
+    def fw_copy(t):
+        reg = gat.at[t, mycols]
+        return tagged(reg, reg, FW, t, other, lb)
 
     seven_halves = gat.at[0, pl.ds(0, 7 * EH)]
-    eight_halves = gat.at[0, pl.ds(0, 8 * EH)]
 
     def p_region(t, m, j):
-        return pg.at[t, pl.ds(*PLANES[j]), chip_rows(m), mycols]
+        return pg.at[t, pl.ds(*PLANES[t][j]), chip_rows(m), mycols]
 
     def p_copy(t, m, j, d):
         reg = p_region(t, m, j)
@@ -165,7 +164,7 @@
     def p_take(t, level):
         for j in SHARES:
             part = members(j)[level]
-            came(pg.at[t, pl.ds(0, PLANES[j][1]), pl.ds(0, RB * len(part)), pl.ds(0, half)], PR + 3 * level + j, t)
+            came(pg.at[t, pl.ds(0, PLANES[t][j][1]), pl.ds(0, RB * len(part)), pl.ds(0, half)], PR + 3 * level + j, t)
             p_pass(t, level + 1, j)
             for m in part:
                 p_over(t, m, j).start()
@@ -441,7 +440,6 @@
             for k, m in ((0, NEAR), (1, FAR[::-1]), (1, NEAR)) if h else ((0, FAR[::-1]),):
                 for q in m:
                     g_copy(t, k, q).start()
-            fw_copy(t, h, 0).start()
 
         sent(rsb.at[t, h], RS + h, t)
 
@@ -475,10 +473,10 @@
     def ev_pass(t):
         r_send(t, BETA, g_sum(t, BETA)[0])
 
-    def ev_fwd(t, h):
-        came(seven_halves, GA + h, t)
-        for m in SEVEN:
-            fw_copy(t, h, m).start()
+    def ev_fwd(t):
+        for h in BOTH:
+            came(seven_halves, GA + h, t)
+        fw_copy(t).start()
 
     def ev_beta(t, s):
         beta = jnp.sqrt(total(t, BETA))
@@ -500,11 +498,10 @@
             vec[t, (s + 1) % 2, pl.ds(pl.multiple_of(first + j, LN), LN)] = new_w(t, s, first + j, LN) * rinv
 
     def ev_vec(t, s):
+        fw_copy(t).wait_recv()
+        vec_rows(t, s, other * half)
+        fw_copy(t).wait_send()
         for h in BOTH:
-            came(eight_halves, FW + h, t)
-        vec_rows(t, s, other * half)
-        for h in BOTH:
-            sent(eight_halves, FW + h, t)
             sent(seven_halves, GA + h, t)
 
     def rel(n, j):
@@ -589,8 +586,7 @@
 
         @pl.when(more)
         def _():
-            ev_fwd(ot, 0)
-            ev_fwd(ot, 1)
+            ev_fwd(ot)
 
         send_part(t, 1, FAR[::-1])
         vec_rows(ot, os, core * half)
@@ -717,7 +713,7 @@
             scratch_shapes=[pltpu.VMEM(shape, F32) for shape in f32_shapes]
             + [pltpu.VMEM((3, 2, mpo, LN, WID), BF16), pltpu.VMEM((3 * PH * mpo, 3 * PH * mpo), BF16)]
             + [pltpu.VMEM(shape, F32) for shape in small]
-            + [dma((KINDS, 2))] * 2
+            + [dma((PR, 2)), dma((KINDS, 2))]
             + [dma((4,))],
             compiler_params=pltpu.CompilerParams(vmem_limit_bytes=63 << 20, has_side_effects=True, collective_id=0),
             name="lanczos",

time: 236 us -> 235 us (level)
  no operation moved by 1% of the time
where the time goes in v8:
time: 235 us
  Pallas kernels  234 us (100%)
    pallas_call x1, Pallas kernels, local_run(): last_rows, sums = call(psi_loc, left_t, right_t, mpo_t)  233 us

profile of v8, /device:TPU:1, one launch (start us, length us, event | category | flops | bytes accessed | tf_op | source)
XLA Modules:
  0.0 235.0 jit_solution(17851707418117923895)
XLA Ops:
  0.6 232.5 %lanczos.1 = (f32[2,8,2,16,128]{4,3,2,1,0:T(8,128)}, f32[2,2,4]{2,1,0:T(2,128)}) custom-call(f32[2,16,2,2,512]{4,3,2,1,0:T(2,128)} %psi_ref.1, f32[20,16,1024]{2,1,0:T(8,128)} %bitcast.4, f32[20,512,1024]{2,1,0:T(8,128)} %bitcast.3, f32[20,2,2,2,2,20]{5,4,3,2,1,0:T(2,128)} %bitcast.5), custom_call_target="tpu_custom_call" | custom-call | tf_op jit(solution)/shard_map/lanczos/pallas_call | solution.py:721
  233.1 1.8 outputs.1

commit v9 on v8

--- a/solution.py
+++ b/solution.py
@@ -28,10 +28,11 @@
 ALPHA, BETA, NORM, FAC = range(4)
 SIZE = FAC + 2
 RS, GA, FW = 0, 2, 4
-PS, PF, FI, AG = range(6, 10)
+PF, FI, AG = range(FW + 1, FW + 4)
 AR = AG + 3
-LS, LF, EX = AR + 3, AR + 6, AR + 9
-PR, LR = EX + 2, EX + 11
+LF, EX = AR + 3, AR + 6
+PS, LS = EX + 1, EX + 2
+PR, LR = PS, PS + 9
 KINDS = LR + 12
 SIDE, MAIN, DIAG = SHARES
 THIRDS = ((0, 4), (4, 3), (7, 3))
@@ -219,6 +220,7 @@
     def ex_over(k):
         return tagged(ex_region(k, False), ex_region(k, False), EX, 1, other, lb)
 
+    others = pl.ds(0, 15)
     group = [(c, m) for c in BOTH for m in EIGHT if c or m]
 
     def flip_core(c):
@@ -232,7 +234,7 @@
             tagged(asend.at[kind, t, 0], gbuf.at[kind, t, core * 8 + eset], AG + kind, t, flip_core(c), gpeer(m)).start()
 
     def g_sum(t, kind):
-        came(gbuf.at[kind, t, pl.ds(0, 15)], AG + kind, t)
+        came(gbuf.at[kind, t, others], AG + kind, t)
         both = [gbuf[kind, t, j] for j in range(RB)]
         return sum(both)[0:1], functools.reduce(jnp.maximum, both)[1:2]
 
@@ -251,7 +253,7 @@
 
     def total(t, kind):
         row = r_sum(t, kind)
-        sent(gbuf.at[kind, t, pl.ds(0, 15)], AG + kind, t)
+        sent(gbuf.at[kind, t, others], AG + kind, t)
         sent(rbuf.at[kind, t, pl.ds(0, 7)], AR + kind, t)
         return mean(row)
 
@@ -331,7 +333,7 @@
     for mn in range(PH):
         planes = [wraw[:, ij // 2, ij % 2, mn // 2, mn % 2, :] for ij in range(PH)]
         wst[pl.ds(mn, mpo, stride=PH), :] = jnp.concatenate(planes + [jnp.zeros((mpo, LN - PH * mpo), F32)], axis=1)
-    w0, w1, w2 = split3(wst[:, :PH * mpo])
+    w0, w1, w2 = split3(wst[:PH * mpo, :PH * mpo])
     none = jnp.zeros_like(w0)
     groups = [jnp.concatenate(g, axis=1) for g in ([w0] * 3, [w1, w1, none], [w2, none, none])]
     wpk[...] = jnp.concatenate(groups, axis=0)
@@ -697,9 +699,9 @@
             (2, PH, LN, bond),
             psi_loc.shape,
             mpo_t.shape,
-            (PH * mpo, LN),
-            (PH * mpo * NX, LN),
-            (PH * mpo * NY, LN),
+            (PH * mpo + EC, LN),
+            (PH * mpo * NX + EC, LN),
+            (PH * mpo * NY + EC, LN),
             (2, 8, EC, WID),
             (2, 2, 7, EH, WID),
             (3, mpo // 4, LN, LN),
@@ -713,7 +715,7 @@
             scratch_shapes=[pltpu.VMEM(shape, F32) for shape in f32_shapes]
             + [pltpu.VMEM((3, 2, mpo, LN, WID), BF16), pltpu.VMEM((3 * PH * mpo, 3 * PH * mpo), BF16)]
             + [pltpu.VMEM(shape, F32) for shape in small]
-            + [dma((PR, 2)), dma((KINDS, 2))]
+            + [dma((LS + 3, 2)), dma((KINDS, 2))]
             + [dma((4,))],
             compiler_params=pltpu.CompilerParams(vmem_limit_bytes=63 << 20, has_side_effects=True, collective_id=0),
             name="lanczos",

time: 235 us -> 235 us (level)
  no operation moved by 1% of the time
where the time goes in v9:
time: 235 us
  Pallas kernels  234 us (100%)
    pallas_call x1, Pallas kernels, local_run(): last_rows, sums = call(psi_loc, left_t, right_t, mpo_t)  232 us

profile of v9, /device:TPU:1, one launch (start us, length us, event | category | flops | bytes accessed | tf_op | source)
XLA Modules:
  0.0 234.8 jit_solution(16920707419632338710)
XLA Ops:
  0.6 232.4 %lanczos.1 = (f32[2,8,2,16,128]{4,3,2,1,0:T(8,128)}, f32[2,2,4]{2,1,0:T(2,128)}) custom-call(f32[2,16,2,2,512]{4,3,2,1,0:T(2,128)} %psi_ref.1, f32[20,16,1024]{2,1,0:T(8,128)} %bitcast.4, f32[20,512,1024]{2,1,0:T(8,128)} %bitcast.3, f32[20,2,2,2,2,20]{5,4,3,2,1,0:T(2,128)} %bitcast.5), custom_call_target="tpu_custom_call" | custom-call | tf_op jit(solution)/shard_map/lanczos/pallas_call | solution.py:723
  233.0 1.8 outputs.1

commit v10 on v9

--- a/solution.py
+++ b/solution.py
@@ -357,7 +357,7 @@
                     l3[k, n, l, rows, cols] = part
             return carry
 
-        lax.fori_loop(0, mpo, split_body, 0)
+        lax.fori_loop(0, mpo, split_body, 0, unroll=4)
 
     def over(phase, part):
         came(l_bytes(phase, RB * len(part)), LF + phase, int(part is FAR))

time: 235 us -> 235 us (level)
  no operation moved by 1% of the time
where the time goes in v10:
time: 235 us
  Pallas kernels  234 us (100%)
    pallas_call x1, Pallas kernels, local_run(): last_rows, sums = call(psi_loc, left_t, right_t, mpo_t)  232 us

profile of v10, /device:TPU:1, one launch (start us, length us, event | category | flops | bytes accessed | tf_op | source)
XLA Modules:
  0.0 234.7 jit_solution(9032041536517122963)
XLA Ops:
  0.6 232.2 %lanczos.1 = (f32[2,8,2,16,128]{4,3,2,1,0:T(8,128)}, f32[2,2,4]{2,1,0:T(2,128)}) custom-call(f32[2,16,2,2,512]{4,3,2,1,0:T(2,128)} %psi_ref.1, f32[20,16,1024]{2,1,0:T(8,128)} %bitcast.4, f32[20,512,1024]{2,1,0:T(8,128)} %bitcast.3, f32[20,2,2,2,2,20]{5,4,3,2,1,0:T(2,128)} %bitcast.5), custom_call_target="tpu_custom_call" | custom-call | tf_op jit(solution)/shard_map/lanczos/pallas_call | solution.py:723
  232.9 1.8 outputs.1

commit v11 on v10

--- a/solution.py
+++ b/solution.py
@@ -357,7 +357,7 @@
                     l3[k, n, l, rows, cols] = part
             return carry
 
-        lax.fori_loop(0, mpo, split_body, 0, unroll=4)
+        lax.fori_loop(0, mpo, split_body, 0, unroll=PH)
 
     def over(phase, part):
         came(l_bytes(phase, RB * len(part)), LF + phase, int(part is FAR))
@@ -420,7 +420,7 @@
                 vec[t, 1, rows] = jnp.zeros((LN, WID), F32)
                 return carry
 
-            lax.fori_loop(0, half // LN, tr_body, 0)
+            lax.fori_loop(0, half // LN, tr_body, 0, unroll=PH)
 
         turn(core * half)
         came(half_psi, PF, t)

time: 235 us -> 235 us (level)
  no operation moved by 1% of the time
where the time goes in v11:
time: 235 us
  Pallas kernels  234 us (100%)
    pallas_call x1, Pallas kernels, local_run(): last_rows, sums = call(psi_loc, left_t, right_t, mpo_t)  233 us

profile of v11, /device:TPU:1, one launch (start us, length us, event | category | flops | bytes accessed | tf_op | source)
XLA Modules:
  0.0 235.0 jit_solution(1054947295586871422)
XLA Ops:
  0.6 232.5 %lanczos.1 = (f32[2,8,2,16,128]{4,3,2,1,0:T(8,128)}, f32[2,2,4]{2,1,0:T(2,128)}) custom-call(f32[2,16,2,2,512]{4,3,2,1,0:T(2,128)} %psi_ref.1, f32[20,16,1024]{2,1,0:T(8,128)} %bitcast.4, f32[20,512,1024]{2,1,0:T(8,128)} %bitcast.3, f32[20,2,2,2,2,20]{5,4,3,2,1,0:T(2,128)} %bitcast.5), custom_call_target="tpu_custom_call" | custom-call | tf_op jit(solution)/shard_map/lanczos/pallas_call | solution.py:723
  233.2 1.8 outputs.1
